TPU v7x, 256 devices: a whole 4x4x8 slice. The times are simulated.
256 devices in a mesh: dp: 128 (over z, x, y), rep: 2 (over core).
Axes of the slice: x: 4, y: 4, z: 8, core: 2. Of those that a mesh axis runs over, the one named last changes fastest.
Arguments:
- queries: bfloat16 [196608, 256], P(('dp', 'rep')), may hold values from -100 to 100
- candidates: bfloat16 [196608, 256], P(('dp', 'rep')), may hold values from -6 to 6
- bucket: int32 [196608, 1], P(('dp', 'rep')), may hold values from 0 to 127, as said below
Outputs:
- query_loss: float32 [196608], P(('dp', 'rep'))
- bucket_loss: float32 [128], P('dp')
Inputs may be any that keep to these rules, and one draw needn't show every extreme that they name: The 768 rows of one device name any bucket at most 12 times; on some device some bucket is named exactly 12 times; a bucket may be named by no row at all.
All inputs are finite; a program needn't handle non-finite values.
Results may differ from a plain program's by a relative error of at most 0.0003.
Values may be sent and summed in bfloat16 or wider, within the bound.
No kernel may reach another device: no remote copies, remote signals or barrier semaphores. Data moves between devices by JAX's collectives and lax.ppermute only.
A program may use at most 64 MiB of HBM per device.

v0:
```python
import math

import jax
import jax.numpy as jnp
from jax import lax
from jax.sharding import PartitionSpec as P

score_scale = 0.0625
neg_large = -1e30


def side_by_side(arrays, axis, split_dim, concat_dim, along):
    columns = [a.reshape(*a.shape[:along], -1) for a in arrays]
    both = jnp.concatenate(columns, axis=along)
    result, at, done = (
        lax.all_to_all(both, axis, split_axis=split_dim, concat_axis=concat_dim, tiled=True),
        0,
        [],
    )
    for a, column in zip(arrays, columns):
        section = result[..., at : at + column.shape[along]]
        done.append(section.reshape(*section.shape[:along], *a.shape[along:]))
        at += column.shape[along]
    return tuple(done)


def joined_along(parts, dim):
    parts = jnp.moveaxis(parts, 0, dim)
    shape = parts.shape
    return parts.reshape(*shape[:dim], shape[dim] * shape[dim + 1], *shape[dim + 2 :])


def copy_for_each(value, axis):
    devices = lax.axis_size(axis)
    return lax.all_to_all(
        jnp.broadcast_to(value[None], (devices, *value.shape)), axis, 0, 0, tiled=True
    )


def gathered_copies(value, axis, dim):
    return joined_along(copy_for_each(value, axis), dim)


def gathered_once(value, axis):
    leaves = jax.tree.leaves(value)
    order = sorted(range(len(leaves)), key=lambda k: -leaves[k].size)
    width = (1, *leaves[order[0]].shape)[-1]
    lines = [
        jnp.pad(leaves[k].reshape(-1), (0, -leaves[k].size % width)).reshape(-1, width)
        for k in order
    ]
    both, at, found = (lax.all_gather(jnp.concatenate(lines), axis), 0, {})
    for k, line in zip(order, lines):
        section = both[:, at : at + len(line)].reshape(len(both), -1)
        found[k] = section[:, : leaves[k].size].reshape(-1, *leaves[k].shape)
        at += len(line)
    numbers = iter(range(len(leaves)))
    return jax.tree.map(lambda _: found[next(numbers)], value)


def joined(value, axis, combine):
    everything = gathered_once(value, axis)
    initial = jax.tree.map(lambda part: part[0], everything)

    def lap(k, so_far):
        return combine(so_far, jax.tree.map(lambda part: part[k], everything))

    return lax.fori_loop(1, lax.axis_size(axis), lap, initial)


def block_stats(qrows, crows, cvalid):
    count = qrows.shape[0]
    blocksize = math.gcd(count, 512)
    columns = crows.shape[0]
    colsize = math.gcd(columns, 2048)
    col_blocks = crows.reshape(columns // colsize, colsize, crows.shape[1])
    valid_blocks = cvalid.reshape(columns // colsize, colsize)

    def one_block(block):

        def step(carry, item):
            top, total = carry
            cpiece, vpiece = item
            scores = (
                lax.dot_general(
                    block, cpiece, (((1,), (1,)), ((), ())), preferred_element_type=jnp.float32
                )
                * score_scale
            )
            scores = jnp.where(vpiece[None, :] > 0, scores, neg_large)
            new_top = jnp.maximum(top, jnp.max(scores, axis=1))
            total = total * jnp.exp(top - new_top) + jnp.sum(
                jnp.exp(scores - new_top[:, None]), axis=1
            )
            return ((new_top, total), None)

        start = (
            jnp.full((block.shape[0],), neg_large, jnp.float32),
            jnp.zeros((block.shape[0],), jnp.float32),
        )
        (top, total), _ = lax.scan(step, start, (col_blocks, valid_blocks))
        return (top, total)

    top, total = lax.map(one_block, qrows.reshape(count // blocksize, blocksize, qrows.shape[1]))
    return (top.reshape(-1), total.reshape(-1))


def combine(first, second):
    top = jnp.maximum(first[0], second[0])
    total = first[1] * jnp.exp(first[0] - top) + second[1] * jnp.exp(second[0] - top)
    return (top, total, first[2] + second[2])


def shards(queries, candidates, bucket):
    peers = lax.axis_size("dp")
    rows_here = queries.shape[0]
    width = queries.shape[1]
    cap = max(2, 2 * rows_here // peers)
    slots = peers * cap
    owner = bucket[:, 0]
    onehot = (owner[:, None] == jnp.arange(peers, dtype=jnp.int32)[None, :]).astype(jnp.int32)
    rank = jnp.sum(jnp.cumsum(onehot, axis=0) * onehot, axis=1) - 1
    slot = owner * cap + rank
    send_q = (
        jnp.zeros((slots, width), jnp.bfloat16).at[slot].set(queries).reshape(peers, cap, width)
    )
    send_c = (
        jnp.zeros((slots, width), jnp.bfloat16).at[slot].set(candidates).reshape(peers, cap, width)
    )
    send_v = jnp.zeros((slots,), jnp.bfloat16).at[slot].set(1.0).reshape(peers, cap)
    recv_q, recv_c, recv_v = side_by_side((send_q, send_c, send_v), "dp", 0, 0, 2)
    recv_q = recv_q.reshape(slots, width)
    recv_c = recv_c.reshape(slots, width)
    recv_v = recv_v.reshape(slots)
    whole_q = gathered_copies(recv_q, "rep", 0)
    part_top, part_total = block_stats(whole_q, recv_c, recv_v)
    own_count = jnp.sum(recv_v.astype(jnp.float32))
    top, total, count = joined((part_top, part_total, own_count), "rep", combine)
    mine = lax.axis_index("rep") * slots
    top = lax.dynamic_slice_in_dim(top, mine, slots, 0)
    total = lax.dynamic_slice_in_dim(total, mine, slots, 0)
    lse = top + jnp.log(total)
    positive = (
        jnp.sum(recv_q.astype(jnp.float32) * recv_c.astype(jnp.float32), axis=1) * score_scale
    )
    count_safe = jnp.maximum(count, 1.0)
    loss = jnp.where(recv_v.astype(jnp.float32) > 0, lse - jnp.log(count_safe) - positive, 0.0)
    returned = lax.all_to_all(
        loss.reshape(peers, cap), "dp", split_axis=0, concat_axis=0, tiled=True
    ).reshape(-1)
    query_loss = returned[slot]
    loss_total = lax.psum(jnp.sum(loss), "rep")
    bucket_loss = (loss_total / count_safe).reshape(1)
    return (query_loss, bucket_loss)


def solution(mesh):
    in_specs = (P(("dp", "rep"), None), P(("dp", "rep"), None), P(("dp", "rep"), None))
    out_specs = (P(("dp", "rep")), P("dp"))
    return jax.shard_map(shards, mesh=mesh, in_specs=in_specs, out_specs=out_specs, check_vma=False)
```

profile of v0, /device:TPU:1, one launch (start us, length us, event | category | flops | bytes accessed | tf_op | source)
XLA Modules:
  0.0 168.8 jit_solution(6644338257363282097)
XLA Ops:
  0.6 0.8 reduce.5
  2.2 8.6 %scatter_custom_fusion.2 = bf16[1536]{0:T(1024)(128)(2,1)S(1)} fusion(s32[768]{0:T(1024)S(1)} %fusion.22, bf16[768]{0:T(1024)(128)(2,1)S(1)} %broadcast.73, bf16[]{:T(256)} %constant.42.clone.1), kind=kCustom, calls=%fused_computation.52 | custom fusion | bytes 3074 | tf_op jit(solution)/shard_map/scatter | solution.py:130
  11.3 6.0 %scatter_custom_fusion.1 = bf16[1536,256]{1,0:T(8,128)(2,1)S(1)} fusion(s32[768]{0:T(1024)S(1)} %fusion.22, bf16[768,256]{1,0:T(8,128)(2,1)} %param.8, bf16[]{:T(256)} %constant.42.clone.1), kind=kCustom, calls=%fused_computation.27 | custom fusion | bytes 786944 | tf_op jit(solution)/shard_map/scatter | solution.py:128
  17.5 6.0 %scatter_custom_fusion = bf16[1536,256]{1,0:T(8,128)(2,1)S(1)} fusion(s32[768]{0:T(1024)S(1)} %fusion.22, bf16[768,256]{1,0:T(8,128)(2,1)} %param.7, bf16[]{:T(256)} %constant.42.clone.1), kind=kCustom, calls=%fused_computation.29 | custom fusion | bytes 786944 | tf_op jit(solution)/shard_map/scatter | solution.py:125
  23.7 1.9 %pad_maximum_fusion = bf16[128,12,513]{2,1,0:T(8,128)(2,1)} fusion(bf16[128,12,1]{2,1,0:T(8,128)(2,1)S(1)} %reshape_reshape.13, bf16[128,12,256]{2,1,0:T(8,128)(2,1)S(1)} %reshape.95, bf16[128,12,256]{2,1,0:T(8,128)(2,1)S(1)} %reshape.94), kind=kLoop, calls=%fused_computation.15 | loop fusion | flops 4727808 | bytes 3151872 | tf_op jit(solution)/shard_map/concatenate | solution.py:14
  25.6 16.5 %all-to-all-start = ((bf16[128,12,513]{2,1,0:T(8,128)(2,1)}), bf16[128,12,513]{2,1,0:T(8,128)(2,1)S(1)}, u32[]{:S(2)}, u32[]{:S(2)}) async-start(bf16[128,12,513]{2,1,0:T(8,128)(2,1)} %pad_maximum_fusion), calls=%async_computation | async-start | bytes 5242880 | tf_op jit(solution)/shard_map/all_to_all | solution.py:16
  42.2 60.0 %all-to-all-done = bf16[128,12,513]{2,1,0:T(8,128)(2,1)S(1)} async-done(((bf16[128,12,513]{2,1,0:T(8,128)(2,1)}), bf16[128,12,513]{2,1,0:T(8,128)(2,1)S(1)}, u32[]{:S(2)}, u32[]{:S(2)}) %all-to-all-start) | async-done | bytes 1575968 | tf_op jit(solution)/shard_map/all_to_all | solution.py:16
  102.7 1.6 fusion.28
  104.3 1.3 reshape_reshape.12
  105.6 1.3 broadcast_in_dim.45
  107.1 9.4 %all_to_all.19 = bf16[2,1536,256]{2,1,0:T(8,128)(2,1)S(1)} all-to-all(bf16[2,1536,256]{2,1,0:T(8,128)(2,1)S(1)} %broadcast_in_dim.46), channel_id=1, replica_groups=mesh['dp'=128,'rep'=2] {'rep'}, dimensions={0} | all-to-all | bytes 3145728 | tf_op jit(solution)/shard_map/all_to_all | solution.py:35
  116.5 12.4 %while.21 = (s32[]{:T(128)}, f32[6,512]{1,0:T(8,128)S(1)}, f32[6,512]{1,0:T(8,128)S(1)}, bf16[6,512,256]{2,1,0:T(8,128)(2,1)S(1)}, bf16[3,512]{1,0:T(4,128)(2,1)...) while((s32[]{:T(128)}, f32[6,512]{1,0:T(8,128)S(1)}, ...), condition=%wide.region_11.12_spmd, body=%wide.region_6.11_spmd.sunk | while | flops 135532544 | bytes 3182897 | solution.py:104
  116.5 1.9 %while.34 = (s32[]{:T(128)}, f32[512]{0:T(512)S(1)}, f32[512]{0:T(512)S(1)}, bf16[3,512]{1,0:T(4,128)(2,1)S(1)}, bf16[3,512,256]{2,1,0:T(8,128)(2,1)S(1)}, /*ind...) while((s32[]{:T(128)}, f32[512]{0:T(512)S(1)}, f32[512]{0:T(512)S(1)}, ...), condition=%wide.region_10.10_spmd.clone, body=%wide.region_7.9_spmd.clone.sunk | while | flops 135532544 | bytes 2650224 | solution.py:101
  118.6 1.9 %while.34 = (s32[]{:T(128)}, f32[512]{0:T(512)S(1)}, f32[512]{0:T(512)S(1)}, bf16[3,512]{1,0:T(4,128)(2,1)S(1)}, bf16[3,512,256]{2,1,0:T(8,128)(2,1)S(1)}, /*ind...) while((s32[]{:T(128)}, f32[512]{0:T(512)S(1)}, f32[512]{0:T(512)S(1)}, ...), condition=%wide.region_10.10_spmd.clone, body=%wide.region_7.9_spmd.clone.sunk | while | flops 135532544 | bytes 2650224 | solution.py:101
  120.7 1.9 %while.34 = (s32[]{:T(128)}, f32[512]{0:T(512)S(1)}, f32[512]{0:T(512)S(1)}, bf16[3,512]{1,0:T(4,128)(2,1)S(1)}, bf16[3,512,256]{2,1,0:T(8,128)(2,1)S(1)}, /*ind...) while((s32[]{:T(128)}, f32[512]{0:T(512)S(1)}, f32[512]{0:T(512)S(1)}, ...), condition=%wide.region_10.10_spmd.clone, body=%wide.region_7.9_spmd.clone.sunk | while | flops 135532544 | bytes 2650224 | solution.py:101
  122.7 1.9 %while.34 = (s32[]{:T(128)}, f32[512]{0:T(512)S(1)}, f32[512]{0:T(512)S(1)}, bf16[3,512]{1,0:T(4,128)(2,1)S(1)}, bf16[3,512,256]{2,1,0:T(8,128)(2,1)S(1)}, /*ind...) while((s32[]{:T(128)}, f32[512]{0:T(512)S(1)}, f32[512]{0:T(512)S(1)}, ...), condition=%wide.region_10.10_spmd.clone, body=%wide.region_7.9_spmd.clone.sunk | while | flops 135532544 | bytes 2650224 | solution.py:101
  124.8 1.9 %while.34 = (s32[]{:T(128)}, f32[512]{0:T(512)S(1)}, f32[512]{0:T(512)S(1)}, bf16[3,512]{1,0:T(4,128)(2,1)S(1)}, bf16[3,512,256]{2,1,0:T(8,128)(2,1)S(1)}, /*ind...) while((s32[]{:T(128)}, f32[512]{0:T(512)S(1)}, f32[512]{0:T(512)S(1)}, ...), condition=%wide.region_10.10_spmd.clone, body=%wide.region_7.9_spmd.clone.sunk | while | flops 135532544 | bytes 2650224 | solution.py:101
  126.9 1.9 %while.34 = (s32[]{:T(128)}, f32[512]{0:T(512)S(1)}, f32[512]{0:T(512)S(1)}, bf16[3,512]{1,0:T(4,128)(2,1)S(1)}, bf16[3,512,256]{2,1,0:T(8,128)(2,1)S(1)}, /*ind...) while((s32[]{:T(128)}, f32[512]{0:T(512)S(1)}, f32[512]{0:T(512)S(1)}, ...), condition=%wide.region_10.10_spmd.clone, body=%wide.region_7.9_spmd.clone.sunk | while | flops 135532544 | bytes 2650224 | solution.py:101
  129.0 1.9 %convert_reduce_fusion = f32[]{:T(128)} fusion(bf16[128,12,513]{2,1,0:T(8,128)(2,1)} %copy-done), kind=kLoop, calls=%fused_computation.17 | loop fusion | flops 3071 | bytes 3076 | tf_op jit(solution)/shard_map/reduce_sum | solution.py:137
  130.9 0.6 pad.4
  131.6 1.9 %all-gather.1 = f32[2,3,3072]{2,1,0:T(4,128)S(1)} all-gather(f32[1,3,3072]{2,1,0:T(4,128)S(1)} %maximum_bitcast_fusion), channel_id=2, replica_groups=mesh['dp'=128,'rep'=2] {'rep'}, dimensions={0}, use_global_device_ids=true | all-gather | bytes 110592 | tf_op jit(solution)/shard_map/all_gather | solution.py:52
  133.6 3.3 %fusion.5 = pred[128,12]{1,0:T(8,128)(4,1)S(1)} fusion(bf16[128,12,513]{2,1,0:T(8,128)(2,1)} %copy-done), kind=kLoop, calls=%fused_computation.19 | loop fusion | flops 3072 | bytes 4608 | tf_op jit(solution)/shard_map/gt | solution.py:147
  137.0 1.9 %multiply_reduce_fusion = f32[128,12]{1,0:T(8,128)S(1)} fusion(bf16[128,12,513]{2,1,0:T(8,128)(2,1)} %copy-done), kind=kLoop, calls=%fused_computation.16 | loop fusion | flops 1571328 | bytes 1579008 | tf_op jit(solution)/shard_map/reduce_sum | solution.py:144
  139.1 0.5 fusion.30
  140.9 0.7 fusion.25
  141.6 0.7 all_to_all.14
  142.4 6.9 %all-to-all-start.2 = ((f32[128,1,12]{2,1,0:T(1,128)}), f32[128,1,12]{2,1,0:T(1,128)S(1)}, u32[]{:S(2)}, u32[]{:S(2)}) async-start(f32[128,1,12]{2,1,0:T(1,128)} %bitcast.15), calls=%async_computation.2 | async-start | bytes 131072 | tf_op jit(solution)/shard_map/all_to_all | solution.py:148
  149.3 3.4 %psum.7 = f32[]{:T(128)} all-reduce(f32[]{:T(128)} %get-tuple-element.139), channel_id=1, replica_groups=mesh['dp'=128,'rep'=2] {'rep'}, use_global_device_ids=true, to_apply=%region_15.16 | all-reduce | flops 1 | bytes 8 | tf_op jit(solution)/shard_map/psum | solution.py:152
  153.4 6.7 %all-to-all-done.2 = f32[128,1,12]{2,1,0:T(1,128)S(1)} async-done(((f32[128,1,12]{2,1,0:T(1,128)}), f32[128,1,12]{2,1,0:T(1,128)S(1)}, u32[]{:S(2)}, u32[]{:S(2)}) %all-to-all-start.2) | async-done | bytes 6176 | tf_op jit(solution)/shard_map/all_to_all | solution.py:148
  160.1 0.5 broadcast.113
  160.6 0.8 reduce.17
  161.5 6.1 %gather_fusion = f32[768]{0:T(1024)} fusion(f32[1536]{0:T(1024)S(1)} %reshape.101, s32[1024]{0:T(1024)S(1)} %pad_clamp_fusion), kind=kCustom, calls=%fused_computation | custom fusion | bytes 9216 | tf_op jit(solution)/shard_map/gather | solution.py:151
  (172 shorter events, 14.2 us)
Async XLA Ops:
  0.6 1.6 copy-start.1
  25.6 76.6 %all-to-all-start = ((bf16[128,12,513]{2,1,0:T(8,128)(2,1)}), bf16[128,12,513]{2,1,0:T(8,128)(2,1)S(1)}, u32[]{:S(2)}, u32[]{:S(2)}) async-start(bf16[128,12,513]{2,1,0:T(8,128)(2,1)} %pad_maximum_fusion), calls=%async_computation | async-start | bytes 5242880 | tf_op jit(solution)/shard_map/all_to_all | solution.py:16
  102.2 2.1 %copy-start = (bf16[128,12,513]{2,1,0:T(8,128)(2,1)}, bf16[128,12,513]{2,1,0:T(8,128)(2,1)S(1)}, u32[]{:S(2)}) copy-start(bf16[128,12,513]{2,1,0:T(8,128)(2,1)S(1)} %all-to-all-done) | copy-start | bytes 4727812
  142.4 17.7 %all-to-all-start.2 = ((f32[128,1,12]{2,1,0:T(1,128)}), f32[128,1,12]{2,1,0:T(1,128)S(1)}, u32[]{:S(2)}, u32[]{:S(2)}) async-start(f32[128,1,12]{2,1,0:T(1,128)} %bitcast.15), calls=%async_computation.2 | async-start | bytes 131072 | tf_op jit(solution)/shard_map/all_to_all | solution.py:148
where the time goes:
time: 169 us
  waiting for transfers between devices  66.7 us (39%)
  local copies, waits for them, and re-layouts  36.4 us (22%)
  starting transfers between devices  23.4 us (14%)
  other arithmetic  16.4 us (10%)
  blocking collectives  14.7 us (9%)
  matrix products  6.25 us (4%)
  between operations  4.06 us (2%)
    all_to_all x1, waiting for transfers between devices, side_by_side(): lax.all_to_all(both, axis, split_axis=split_dim, concat_axis=concat_dim,...  60 us
    all_to_all x1, starting transfers between devices, side_by_side(): lax.all_to_all(both, axis, split_axis=split_dim, concat_axis=concat_dim,...  16.5 us
    all_to_all x1, blocking collectives, copy_for_each(): lax.all_to_all(jnp.broadcast_to(value[None], (devices, *value.shape)), ax...  9.42 us
    scatter x1, local copies, waits for them, and re-layouts, shards(): jnp.zeros((slots,), jnp.bfloat16).at[slot].set(1.0).reshape(peers, cap)  8.62 us
    all_to_all x1, starting transfers between devices, shards(): lax.all_to_all(loss.reshape(peers, cap), 'dp', split_axis=0, concat_axis=...  6.91 us
    all_to_all x1, waiting for transfers between devices, shards(): lax.all_to_all(loss.reshape(peers, cap), 'dp', split_axis=0, concat_axis=...  6.7 us
    dot_general x18, matrix products, step(): lax.dot_general(block, cpiece, (((1,), (1,)), ((), ())), preferred_elemen...  6.25 us
    gather x1, local copies, waits for them, and re-layouts, shards(): query_loss = returned[slot]  6.15 us
  transfers between devices with their start and end apart: 2, of which 2 were waited for; matrix products, arithmetic and copies ran while one was open for 0% of the time, Pallas kernels for 0%

commit v1 on v0

v1 whole, which is shorter than its diff:
```python
import math

import jax
import jax.numpy as jnp
from jax import lax
from jax.experimental import pallas as pl
from jax.experimental.pallas import tpu as pltpu
from jax.sharding import PartitionSpec as P

ROWS = 768
WIDTH = 256
HALF = 128
PEERS = 128
CAP = 12
SLOTS = PEERS * CAP
MAIN = PEERS * 8
REST = PEERS * 4
ABSENT = 64.0
NEG = -1e30
LN2 = math.log(2.0)
TO_LOG2 = 0.0625 / LN2

F32 = jnp.float32
BF16 = jnp.bfloat16
VMEM = pl.BlockSpec(memory_space=pltpu.VMEM)


def iota(shape, dim):
    return lax.broadcasted_iota(jnp.int32, shape, dim)


def dot_nn(a, b):
    return lax.dot_general(a, b, (((1,), (0,)), ((), ())), preferred_element_type=F32)


def dot_nt(a, b):
    return lax.dot_general(a, b, (((1,), (1,)), ((), ())), preferred_element_type=F32)


def dot_tn(a, b):
    return lax.dot_general(a, b, (((0,), (0,)), ((), ())), preferred_element_type=F32)


def ranks(b):
    blocks = ROWS // 128
    row = iota((128, 128), 0)
    hot = [(row == b[:, j * 128 : (j + 1) * 128]).astype(F32) for j in range(blocks)]
    stack = jnp.concatenate(hot, axis=0).astype(BF16)
    upper = (iota((128, 256), 0) < iota((128, 256), 1)).astype(F32).astype(BF16)
    both = dot_nn(stack, upper)
    before = jnp.zeros((128, 128), F32)
    rank = []
    for j in range(blocks):
        at = both[j * 128 : (j + 1) * 128]
        rank.append(jnp.sum(hot[j] * (at[:, :128] + before), axis=0, keepdims=True))
        before = before + at[:, 128:]
    return jnp.concatenate(rank, axis=1).astype(jnp.int32), before


def pack_kernel(b_ref, q_ref, c_ref, out_ref):
    b = b_ref[...]
    rank, count = ranks(b)
    main_key = jnp.where(rank < 8, b * 8 + rank, -1)
    rest_key = jnp.where(rank >= 8, b * 8 + rank - 8, -1)
    q = q_ref[...]
    c = c_ref[...]
    step = 32
    for p0 in range(0, PEERS, step):
        n = step * 8
        ids = iota((n, ROWS), 0) + p0 * 8
        main = (ids == main_key).astype(F32).astype(BF16)
        rest = ((ids & ~4) == rest_key).astype(F32).astype(BF16)
        c_main = dot_nn(main, c).reshape(step, 8, WIDTH)
        q_main = dot_nn(main, q).reshape(step, 8, WIDTH)
        c_rest = dot_nn(rest, c).reshape(step, 8, WIDTH)
        q_rest = dot_nn(rest, q).reshape(step, 8, WIDTH)
        slot = iota((step, 8, HALF), 1)
        lane = iota((step, 8, HALF), 2)
        have = jnp.broadcast_to(count[p0 : p0 + step].astype(jnp.int32)[:, None, :], (step, 8, HALF))
        c_lo = jnp.where((lane == 0) & (slot >= have), ABSENT, c_main[:, :, :HALF])
        r_lo = jnp.where(
            slot < 4,
            jnp.where((lane == 0) & (slot + 8 >= have), ABSENT, c_rest[:, :, :HALF]),
            q_rest[:, :, :HALF],
        )
        r_hi = jnp.where(slot < 4, c_rest[:, :, HALF:], q_rest[:, :, HALF:])
        out_ref[p0 : p0 + step, 0:16, :] = jnp.concatenate(
            [c_lo, c_main[:, :, HALF:]], axis=1
        ).astype(BF16)
        out_ref[p0 : p0 + step, 16:32, :] = jnp.concatenate([r_lo, r_hi], axis=1).astype(BF16)
        out_ref[p0 : p0 + step, 32:48, :] = jnp.concatenate(
            [q_main[:, :, :HALF], q_main[:, :, HALF:]], axis=1
        ).astype(BF16)


def unpack_kernel(in_ref, q_ref, c_ref):
    def main_rows(at):
        tile = in_ref[:, at : at + 16, :].astype(F32)
        lo = tile[:, :8, :].reshape(MAIN, HALF)
        hi = tile[:, 8:, :].reshape(MAIN, HALF)
        return lo.astype(BF16), hi.astype(BF16)

    c_lo, c_hi = main_rows(0)
    c_ref[0:MAIN, :HALF] = c_lo
    c_ref[0:MAIN, HALF:] = c_hi
    q_lo, q_hi = main_rows(32)
    q_ref[0:MAIN, :HALF] = q_lo
    q_ref[0:MAIN, HALF:] = q_hi
    tile = in_ref[:, 16:32, :].astype(F32)
    first = iota((PEERS // 2, 8, HALF), 1) < 4
    for half in range(2):
        part = tile[:, half * 8 : half * 8 + 8, :].reshape(PEERS // 2, 2, 8, HALF)
        even = part[:, 0]
        odd = part[:, 1]
        c_part = jnp.where(first, even, pltpu.roll(odd, 4, 1))
        q_part = jnp.where(first, pltpu.roll(even, 4, 1), odd)
        c_ref[MAIN:SLOTS, half * HALF : (half + 1) * HALF] = c_part.reshape(REST, HALF).astype(BF16)
        q_ref[MAIN:SLOTS, half * HALF : (half + 1) * HALF] = q_part.reshape(REST, HALF).astype(BF16)


COLS = 256
CHUNK = 512


def scores_of(q_ref, c_ref, bias_ref, t_ref, done):
    def fill(k, total):
        at = pl.multiple_of(k * CHUNK, CHUNK)
        absent = c_ref[pl.ds(at, CHUNK), 0:1].astype(F32) == ABSENT
        bias_ref[pl.ds(at, CHUNK), :] = jnp.broadcast_to(
            jnp.where(absent, NEG, 0.0), (CHUNK, HALF)
        )
        return total + jnp.sum(jnp.where(absent, 0.0, 1.0), axis=0, keepdims=True)

    count = jnp.zeros((1, 1), F32)
    for k in range(SLOTS // CHUNK):
        count = fill(k, count)

    for j in range(SLOTS // COLS):
        q = q_ref[j * COLS : (j + 1) * COLS, :]
        top = jnp.full((8, COLS), NEG * 2, F32)
        for k in range(SLOTS // CHUNK):
            s = dot_nt(c_ref[k * CHUNK : (k + 1) * CHUNK, :], q)
            bias = bias_ref[k * CHUNK : (k + 1) * CHUNK, :]
            t = s * TO_LOG2 + jnp.concatenate([bias, bias], axis=1)
            t_ref[k * CHUNK : (k + 1) * CHUNK, :] = t
            top = jnp.maximum(top, jnp.max(t.reshape(CHUNK // 8, 8, COLS), axis=0))
        top = jnp.max(top, axis=0, keepdims=True)
        total = jnp.zeros((8, COLS), F32)
        for k in range(SLOTS // CHUNK):
            e = jnp.exp2(t_ref[k * CHUNK : (k + 1) * CHUNK, :] - top)
            total = total + jnp.sum(e.reshape(CHUNK // 8, 8, COLS), axis=0)
        done(j, top, jnp.sum(total, axis=0, keepdims=True))
    return count


def own_kernel(q_ref, c_ref, top_ref, total_ref, count_ref, bias_ref, t_ref):
    def done(j, top, total):
        top_ref[:, j * COLS : (j + 1) * COLS] = top
        total_ref[:, j * COLS : (j + 1) * COLS] = total

    count = scores_of(q_ref, c_ref, bias_ref, t_ref, done)
    count_ref[...] = jnp.broadcast_to(count, (1, 128))


def other_kernel(
    q_ref, own_ref, c_ref, top_ref, total_ref, count_ref, out_ref, sum_ref, n_ref, bias_ref, t_ref, lse_ref
):
    def done(j, top, total):
        top0 = top_ref[:, j * COLS : (j + 1) * COLS]
        total0 = total_ref[:, j * COLS : (j + 1) * COLS]
        new = jnp.maximum(top0, top)
        both = total0 * jnp.exp2(top0 - new) + total * jnp.exp2(top - new)
        lse_ref[:, j * COLS : (j + 1) * COLS] = new * LN2 + jnp.log(both)

    count = scores_of(q_ref, c_ref, bias_ref, t_ref, done) + count_ref[:, 0:1]
    n = jnp.maximum(jnp.broadcast_to(count, (1, 128)), 1.0)
    log_n = jnp.log(n)
    lines = [lse_ref[:, t * 128 : (t + 1) * 128] - log_n for t in range(CAP)]
    lane = iota((1, 128), 1)
    for u in range(PEERS // 8):
        a = lines[u // 2]
        if u % 2:
            a = pltpu.roll(a, 64, 1)
        r = lines[8 + u // 4]
        shift = (64 - 32 * (u % 4)) % 128
        if shift:
            r = pltpu.roll(r, shift, 1)
        line = jnp.where(lane < 64, a, jnp.where(lane < 96, r, 0.0))
        out_ref[u * 8 : (u + 1) * 8, :] = jnp.broadcast_to(line, (8, 128))
    total = lines[0]
    for line in lines[1:]:
        total = total + line
    total = jnp.sum(total, axis=1, keepdims=True)
    total = jnp.where(count > 0, total, 0.0)
    pos = jnp.zeros((8, WIDTH), F32)
    for k in range(SLOTS // CHUNK):
        at = slice(k * CHUNK, (k + 1) * CHUNK)
        both = q_ref[at, :].astype(F32) * own_ref[at, :].astype(F32)
        pos = pos + jnp.sum(both.reshape(CHUNK // 8, 8, WIDTH), axis=0)
    pos = jnp.sum(jnp.sum(pos, axis=0, keepdims=True), axis=1, keepdims=True)
    sum_ref[...] = jnp.broadcast_to(total - pos * 0.0625, (1, 128))
    n_ref[...] = n


def positive_kernel(b_ref, q_ref, c_ref, pos_ref, rank_ref):
    rank, _ = ranks(b_ref[...])
    rank_ref[...] = rank
    both = q_ref[...].astype(F32) * c_ref[...].astype(F32)
    hi = both.astype(BF16)
    lo = (both - hi.astype(F32)).astype(BF16)
    ones = jnp.ones((8, WIDTH), BF16)
    pos_ref[...] = ((dot_nt(ones, hi) + dot_nt(ones, lo)) * 0.0625)[0:1]


def finish_kernel(at_ref, b_ref, rank_ref, pos_ref, back_ref, out_ref):
    me = at_ref[0]
    b = b_ref[...]
    rank = rank_ref[...]
    hot = (iota((PEERS, ROWS), 0) == b).astype(F32).astype(BF16)
    x = back_ref[...]
    hi = x.astype(BF16)
    left = x - hi.astype(F32)
    mid = left.astype(BF16)
    lo = (left - mid.astype(F32)).astype(BF16)
    picked = (dot_tn(hi, hot) + dot_tn(mid, hot)) + dot_tn(lo, hot)
    eighth = me & 7
    lane = jnp.where(rank < 8, eighth * 8 + rank, 64 + eighth * 4 + rank - 8)
    mine = jnp.sum(jnp.where(iota((128, ROWS), 0) == lane, picked, 0.0), axis=0, keepdims=True)
    out_ref[...] = mine - pos_ref[...]


def shards(queries, candidates, bucket):
    b = bucket.reshape(1, ROWS)
    packed = pl.pallas_call(
        pack_kernel,
        out_shape=jax.ShapeDtypeStruct((PEERS, 48, HALF), BF16),
        in_specs=[VMEM] * 3,
        out_specs=VMEM,
        name="pack",
    )(b, queries, candidates)
    received = lax.all_to_all(packed, "dp", split_axis=0, concat_axis=0, tiled=True)
    pos, rank = pl.pallas_call(
        positive_kernel,
        out_shape=(
            jax.ShapeDtypeStruct((1, ROWS), F32),
            jax.ShapeDtypeStruct((1, ROWS), jnp.int32),
        ),
        in_specs=[VMEM] * 3,
        out_specs=(VMEM, VMEM),
        name="positive",
    )(b, queries, candidates)
    slots = jax.ShapeDtypeStruct((SLOTS, WIDTH), BF16)
    own_q, own_c = pl.pallas_call(
        unpack_kernel,
        out_shape=(slots, slots),
        in_specs=[VMEM],
        out_specs=(VMEM, VMEM),
        name="unpack",
    )(received)
    other_c = lax.ppermute(own_c, "rep", [(0, 1), (1, 0)])
    line = jax.ShapeDtypeStruct((1, SLOTS), F32)
    short = jax.ShapeDtypeStruct((1, 128), F32)
    scratch = [pltpu.VMEM((SLOTS, HALF), F32), pltpu.VMEM((SLOTS, COLS), F32)]
    top, total, count = pl.pallas_call(
        own_kernel,
        out_shape=(line, line, short),
        in_specs=[VMEM] * 2,
        out_specs=(VMEM,) * 3,
        scratch_shapes=scratch,
        name="own",
    )(own_q, own_c)
    back, loss_sum, n = pl.pallas_call(
        other_kernel,
        out_shape=(jax.ShapeDtypeStruct((PEERS, 128), F32), short, short),
        in_specs=[VMEM] * 6,
        out_specs=(VMEM,) * 3,
        scratch_shapes=scratch + [pltpu.VMEM((1, SLOTS), F32)],
        name="other",
    )(own_q, own_c, other_c, top, total, count)
    returned = lax.all_to_all(back, "dp", split_axis=0, concat_axis=0, tiled=True)
    loss_total = lax.psum(loss_sum[0, 0], "rep")
    bucket_loss = (loss_total / n[0, 0]).reshape(1)
    me = lax.axis_index("dp").astype(jnp.int32).reshape(1)
    query_loss = pl.pallas_call(
        finish_kernel,
        out_shape=jax.ShapeDtypeStruct((1, ROWS), F32),
        in_specs=[pl.BlockSpec(memory_space=pltpu.SMEM)] + [VMEM] * 4,
        out_specs=VMEM,
        name="finish",
    )(me, b, rank, pos, returned)
    return (query_loss.reshape(ROWS), bucket_loss)


def solution(mesh):
    in_specs = (P(("dp", "rep"), None), P(("dp", "rep"), None), P(("dp", "rep"), None))
    out_specs = (P(("dp", "rep")), P("dp"))
    return jax.shard_map(shards, mesh=mesh, in_specs=in_specs, out_specs=out_specs, check_vma=False)
```

time: 169 us -> 101 us (0.60)
  waiting for transfers between devices: 66.7 us -> 4.22 us
  blocking collectives: 14.7 us -> 58.7 us
  local copies, waits for them, and re-layouts: 36.4 us -> 1.51 us
  Pallas kernels: 0 us -> 21.4 us
  other arithmetic: 16.4 us -> 1.29 us
  starting transfers between devices: 23.4 us -> 10.1 us
  matrix products: 6.25 us -> 0 us
    all_to_all x2 -> x1, waiting for transfers between devices: 66.7 us -> 4.22 us  [shards(): lax.all_to_all(back, 'dp', split_axis=0, concat_axis=0, tiled=True)]
    all_to_all x1, blocking collectives: 9.42 us -> 55.6 us  [shards(): lax.all_to_all(packed, 'dp', split_axis=0, concat_axis=0, tiled=True)]
    pallas_call x0 -> x6, Pallas kernels: none -> 21.4 us  [the longest x1 5.3 us: shards(): pl.pallas_call(other_kernel, out_shape=(jax.ShapeDtypeStruct((PEERS, 128)...]
    scatter x3 -> x0, local copies, waits for them, and re-layouts: 20.7 us -> none  [the longest x1 8.62 us: shards(): jnp.zeros((slots,), jnp.bfloat16).at[slot].set(1.0).reshape(peers, cap)]
    all_to_all x2 -> x1, starting transfers between devices: 23.4 us -> 6.17 us  [shards(): lax.all_to_all(back, 'dp', split_axis=0, concat_axis=0, tiled=True)]
    reduce_sum x22 -> x0, other arithmetic: 8.39 us -> none  [the longest x18 3.53 us: step(): jnp.sum(jnp.exp(scores - new_top[:, None]), axis=1)]
    dot_general x18 -> x0, matrix products: 6.25 us -> none  [step(): lax.dot_general(block, cpiece, (((1,), (1,)), ((), ())), preferred_elemen...]
    gather x1 -> x0, local copies, waits for them, and re-layouts: 6.15 us -> none  [shards(): query_loss = returned[slot]]
  transfers between devices with their start and end apart: 2 -> 2, of which waited for: 2 -> 1; matrix products, arithmetic and copies ran while one was open for 0% -> 0% of each run, Pallas kernels for 0% -> 7%
where the time goes in v1:
time: 101 us; the launch traced here: 100 us
  blocking collectives  58.7 us (58%)
  Pallas kernels  21.4 us (21%)
  starting transfers between devices  10.1 us (10%)
  waiting for transfers between devices  4.22 us (4%)
  between operations  3.1 us (3%)
  local copies, waits for them, and re-layouts  1.51 us (1%)
  other arithmetic  1.29 us (1%)
    all_to_all x1, blocking collectives, shards(): lax.all_to_all(packed, 'dp', split_axis=0, concat_axis=0, tiled=True)  55.6 us
    all_to_all x1, starting transfers between devices, shards(): lax.all_to_all(back, 'dp', split_axis=0, concat_axis=0, tiled=True)  6.17 us
    pallas_call x1, Pallas kernels, shards(): pl.pallas_call(other_kernel, out_shape=(jax.ShapeDtypeStruct((PEERS, 128)...  5.3 us
    pallas_call x1, Pallas kernels, shards(): pl.pallas_call(own_kernel, out_shape=(line, line, short), in_specs=[VMEM]...  4.78 us
    pallas_call x1, Pallas kernels, shards(): pl.pallas_call(pack_kernel, out_shape=jax.ShapeDtypeStruct((PEERS, 48, HA...  4.44 us
    all_to_all x1, waiting for transfers between devices, shards(): lax.all_to_all(back, 'dp', split_axis=0, concat_axis=0, tiled=True)  4.22 us
    ppermute x1, starting transfers between devices, shards(): other_c = lax.ppermute(own_c, 'rep', [(0, 1), (1, 0)])  3.95 us
    psum x1, blocking collectives, shards(): loss_total = lax.psum(loss_sum[0, 0], 'rep')  3.09 us
  transfers between devices with their start and end apart: 2, of which 1 were waited for; matrix products, arithmetic and copies ran while one was open for 0% of the time, Pallas kernels for 7%

profile of v1, /device:TPU:1, one launch (start us, length us, event | category | flops | bytes accessed | tf_op | source)
XLA Modules:
  0.0 100.3 jit_solution(13510412526342821439)
XLA Ops:
  0.6 4.4 %pack.1 = bf16[128,48,128]{2,1,0:T(8,128)(2,1)} custom-call(s32[1,768]{1,0:T(1,128)} %bitcast.13, bf16[768,256]{1,0:T(8,128)(2,1)} %q_ref.3, bf16[768,256]{1,0:T(8,128)(2,1)} %c_ref.3), custom_call_target="tpu_custom_call" | custom-call | tf_op jit(solution)/shard_map/pack/pallas_call | solution.py:234
  5.1 55.6 %all_to_all.16.in_ref = bf16[128,48,128]{2,1,0:T(8,128)(2,1)} all-to-all(bf16[128,48,128]{2,1,0:T(8,128)(2,1)} %pack.1), channel_id=1, replica_groups=mesh['dp'=128,'rep'=2] {'dp'}, dimensions={0} | all-to-all | bytes 3145728 | tf_op jit(solution)/shard_map/all_to_all | solution.py:241
  60.7 2.9 %unpack.1 = (bf16[1536,256]{1,0:T(8,128)(2,1)}, bf16[1536,256]{1,0:T(8,128)(2,1)}) custom-call(bf16[128,48,128]{2,1,0:T(8,128)(2,1)} %all_to_all.16.in_ref), custom_call_target="tpu_custom_call" | custom-call | tf_op jit(solution)/shard_map/unpack/pallas_call | solution.py:253
  63.6 3.9 %collective-permute-start = (bf16[1536,256]{1,0:T(8,128)(2,1)}, bf16[1536,256]{1,0:T(8,128)(2,1)S(1)}, u32[]{:S(2)}, u32[]{:S(2)}) collective-permute-start(bf16[1536,256]{1,0:T(8,128)(2,1)} %get-tuple-element.15.c_ref.own_ref), channel_id=1, source_target_pairs={{0,1},{1,0},{2,3},{3,2},{4,5},{5,4},{6,7},{7,6},{8,9},{9,8},{10,11... | collective-permute-start | bytes 2359304 | tf_op jit(solution)/shard_map/ppermute | solution.py:260
  67.5 4.8 %own.1 = (f32[1,1536]{1,0:T(1,128)}, f32[1,1536]{1,0:T(1,128)}, f32[1,128]{1,0:T(1,128)}) custom-call(bf16[1536,256]{1,0:T(8,128)(2,1)} %get-tuple-element.14.q_ref, bf16[1536,256]{1,0:T(8,128)(2,1)} %get-tuple-element.15.c_ref.own_ref), custom_call_target="tpu_custom_call" | custom-call | tf_op jit(solution)/shard_map/own/pallas_call | solution.py:264
  72.3 0.0 collective-permute-done.c_ref
  72.3 0.0 copy-start
  72.3 0.9 copy-done
  73.2 5.3 %other.1 = (f32[128,128]{1,0:T(8,128)}, f32[1,128]{1,0:T(1,128)}, f32[1,128]{1,0:T(1,128)}) custom-call(bf16[1536,256]{1,0:T(8,128)(2,1)} %get-tuple-element.14.q_ref, bf16[1536,256]{1,0:T(8,128)(2,1)} %get-tuple-element.15.c_ref.own_ref, bf16[1536,256]{1,0:T(8,128)(2,1)} %copy-done, f32[1,1536]{1,0:T(1,128)} %get-tuple-element.16.top_ref, ...), custom_call_target="tpu_custom_call" | custom-call | tf_op jit(solution)/shard_map/other/pallas_call | solution.py:272
  78.5 6.2 %all-to-all-start.1 = ((f32[128,1,128]{2,1,0:T(1,128)}), f32[128,1,128]{2,1,0:T(1,128)S(1)}, u32[]{:S(2)}, u32[]{:S(2)}) async-start(f32[128,1,128]{2,1,0:T(1,128)} %bitcast.12), calls=%async_computation.1 | async-start | bytes 131072 | tf_op jit(solution)/shard_map/all_to_all | solution.py:280
  84.7 2.1 %positive.1 = (f32[1,768]{1,0:T(1,128)}, s32[1,768]{1,0:T(1,128)}) custom-call(s32[1,768]{1,0:T(1,128)} %bitcast.14, bf16[768,256]{1,0:T(8,128)(2,1)} %q_ref.3, bf16[768,256]{1,0:T(8,128)(2,1)} %c_ref.3), custom_call_target="tpu_custom_call" | custom-call | tf_op jit(solution)/shard_map/positive/pallas_call | solution.py:242
  86.8 3.1 %psum.7 = f32[]{:T(128)} all-reduce(f32[]{:T(128)} %bitcast.17), channel_id=1, replica_groups=mesh['dp'=128,'rep'=2] {'rep'}, use_global_device_ids=true, to_apply=%region_0.0 | all-reduce | flops 1 | bytes 8 | tf_op jit(solution)/shard_map/psum | solution.py:281
  91.2 4.2 %all-to-all-done.1 = f32[128,1,128]{2,1,0:T(1,128)S(1)} async-done(((f32[128,1,128]{2,1,0:T(1,128)}), f32[128,1,128]{2,1,0:T(1,128)S(1)}, u32[]{:S(2)}, u32[]{:S(2)}) %all-to-all-start.1) | async-done | bytes 65568 | tf_op jit(solution)/shard_map/all_to_all | solution.py:280
  95.5 0.0 copy-start.1
  95.5 0.6 copy-done.1
  96.1 1.8 %finish.1 = f32[1,768]{1,0:T(1,128)} custom-call(s32[1]{0:T(128)} %bitcast.at_ref, s32[1,768]{1,0:T(1,128)} %bitcast.15, s32[1,768]{1,0:T(1,128)} %get-tuple-element.12.rank_ref, f32[1,768]{1,0:T(1,128)} %get-tuple-element.13.pos_ref, f32[128,128]{1,0:T(8,128)} %bitcast.11), custom_call_target="tpu_custom_call" | custom-call | tf_op jit(solution)/shard_map/finish/pallas_call | solution.py:284
  97.9 1.3 %reduce = f32[768]{0:T(1024)} reduce(f32[1,768]{1,0:T(1,128)} %finish.1, f32[]{:T(128)} %constant.6), dimensions={0}, to_apply=%pallas_call.43.reduce_sub_computation | reduce | bytes 6148 | tf_op jit(solution)/shard_map/finish/pallas_call | solution.py:284
Async XLA Ops:
  63.6 8.7 %collective-permute-start = (bf16[1536,256]{1,0:T(8,128)(2,1)}, bf16[1536,256]{1,0:T(8,128)(2,1)S(1)}, u32[]{:S(2)}, u32[]{:S(2)}) collective-permute-start(bf16[1536,256]{1,0:T(8,128)(2,1)} %get-tuple-element.15.c_ref.own_ref), channel_id=1, source_target_pairs={{0,1},{1,0},{2,3},{3,2},{4,5},{5,4},{6,7},{7,6},{8,9},{9,8},{10,11... | collective-permute-start | bytes 2359304 | tf_op jit(solution)/shard_map/ppermute | solution.py:260
  72.3 0.9 copy-start
  78.5 17.0 %all-to-all-start.1 = ((f32[128,1,128]{2,1,0:T(1,128)}), f32[128,1,128]{2,1,0:T(1,128)S(1)}, u32[]{:S(2)}, u32[]{:S(2)}) async-start(f32[128,1,128]{2,1,0:T(1,128)} %bitcast.12), calls=%async_computation.1 | async-start | bytes 131072 | tf_op jit(solution)/shard_map/all_to_all | solution.py:280
  95.5 0.6 copy-start.1

commit v2 on v1

--- a/solution.py
+++ b/solution.py
@@ -93,7 +93,7 @@
         ).astype(BF16)
 
 
-def unpack_kernel(in_ref, q_ref, c_ref):
+def unpack_kernel(in_ref, q_ref, c_ref, send_ref):
     def main_rows(at):
         tile = in_ref[:, at : at + 16, :].astype(F32)
         lo = tile[:, :8, :].reshape(MAIN, HALF)
@@ -116,6 +116,7 @@
         q_part = jnp.where(first, pltpu.roll(even, 4, 1), odd)
         c_ref[MAIN:SLOTS, half * HALF : (half + 1) * HALF] = c_part.reshape(REST, HALF).astype(BF16)
         q_ref[MAIN:SLOTS, half * HALF : (half + 1) * HALF] = q_part.reshape(REST, HALF).astype(BF16)
+    send_ref[...] = c_ref[...]
 
 
 COLS = 256
@@ -229,11 +230,15 @@
     out_ref[...] = mine - pos_ref[...]
 
 
+def on_chip(x):
+    return pltpu.with_memory_space_constraint(x, pltpu.VMEM)
+
+
 def shards(queries, candidates, bucket):
     b = bucket.reshape(1, ROWS)
     packed = pl.pallas_call(
         pack_kernel,
-        out_shape=jax.ShapeDtypeStruct((PEERS, 48, HALF), BF16),
+        out_shape=pltpu.VMEM((PEERS, 48, HALF), BF16),
         in_specs=[VMEM] * 3,
         out_specs=VMEM,
         name="pack",
@@ -242,24 +247,24 @@
     pos, rank = pl.pallas_call(
         positive_kernel,
         out_shape=(
-            jax.ShapeDtypeStruct((1, ROWS), F32),
-            jax.ShapeDtypeStruct((1, ROWS), jnp.int32),
+            pltpu.VMEM((1, ROWS), F32),
+            pltpu.VMEM((1, ROWS), jnp.int32),
         ),
         in_specs=[VMEM] * 3,
         out_specs=(VMEM, VMEM),
         name="positive",
     )(b, queries, candidates)
-    slots = jax.ShapeDtypeStruct((SLOTS, WIDTH), BF16)
-    own_q, own_c = pl.pallas_call(
+    slots = pltpu.VMEM((SLOTS, WIDTH), BF16)
+    own_q, own_c, sent_c = pl.pallas_call(
         unpack_kernel,
-        out_shape=(slots, slots),
+        out_shape=(slots, slots, jax.ShapeDtypeStruct((SLOTS, WIDTH), BF16)),
         in_specs=[VMEM],
-        out_specs=(VMEM, VMEM),
+        out_specs=(VMEM,) * 3,
         name="unpack",
-    )(received)
-    other_c = lax.ppermute(own_c, "rep", [(0, 1), (1, 0)])
-    line = jax.ShapeDtypeStruct((1, SLOTS), F32)
-    short = jax.ShapeDtypeStruct((1, 128), F32)
+    )(on_chip(received))
+    other_c = lax.ppermute(sent_c, "rep", [(0, 1), (1, 0)])
+    line = pltpu.VMEM((1, SLOTS), F32)
+    short = pltpu.VMEM((1, 128), F32)
     scratch = [pltpu.VMEM((SLOTS, HALF), F32), pltpu.VMEM((SLOTS, COLS), F32)]
     top, total, count = pl.pallas_call(
         own_kernel,
@@ -268,7 +273,7 @@
         out_specs=(VMEM,) * 3,
         scratch_shapes=scratch,
         name="own",
-    )(own_q, own_c)
+    )(on_chip(own_q), on_chip(own_c))
     back, loss_sum, n = pl.pallas_call(
         other_kernel,
         out_shape=(jax.ShapeDtypeStruct((PEERS, 128), F32), short, short),
@@ -276,7 +281,7 @@
         out_specs=(VMEM,) * 3,
         scratch_shapes=scratch + [pltpu.VMEM((1, SLOTS), F32)],
         name="other",
-    )(own_q, own_c, other_c, top, total, count)
+    )(*[on_chip(x) for x in (own_q, own_c, other_c, top, total, count)])
     returned = lax.all_to_all(back, "dp", split_axis=0, concat_axis=0, tiled=True)
     loss_total = lax.psum(loss_sum[0, 0], "rep")
     bucket_loss = (loss_total / n[0, 0]).reshape(1)
@@ -287,7 +292,7 @@
         in_specs=[pl.BlockSpec(memory_space=pltpu.SMEM)] + [VMEM] * 4,
         out_specs=VMEM,
         name="finish",
-    )(me, b, rank, pos, returned)
+    )(me, b, on_chip(rank), on_chip(pos), on_chip(returned))
     return (query_loss.reshape(ROWS), bucket_loss)
 
 

time: 101 us -> 94.6 us (0.937)
  Pallas kernels: 21.4 us -> 14.5 us
  waiting for transfers between devices: 4.22 us -> 5.57 us
    pallas_call x3, Pallas kernels: 9.48 us -> 6.23 us  [the longest x1 3.28 us: shards(): pl.pallas_call(pack_kernel, out_shape=pltpu.VMEM((PEERS, 48, HALF), BF16)...]
    pallas_call x1, Pallas kernels: 4.78 us -> 2.92 us  [shards(): pl.pallas_call(own_kernel, out_shape=(line, line, short), in_specs=[VMEM]...]
    pallas_call x1, Pallas kernels: 5.3 us -> 3.69 us  [shards(): pl.pallas_call(other_kernel, out_shape=(jax.ShapeDtypeStruct((PEERS, 128)...]
    all_to_all x1, waiting for transfers between devices: 4.22 us -> 5.57 us  [shards(): lax.all_to_all(back, 'dp', split_axis=0, concat_axis=0, tiled=True)]
  transfers between devices with their start and end apart: 2 -> 2, of which waited for: 1 -> 1; matrix products, arithmetic and copies ran while one was open for 0% -> 0% of each run, Pallas kernels for 7% -> 5%
where the time goes in v2:
time: 94.6 us; the launch traced here: 94.2 us
  blocking collectives  58.3 us (62%)
  Pallas kernels  14.5 us (15%)
  starting transfers between devices  10.1 us (11%)
  waiting for transfers between devices  5.57 us (6%)
  between operations  2.49 us (3%)
  local copies, waits for them, and re-layouts  2.02 us (2%)
  other arithmetic  1.28 us (1%)
    all_to_all x1, blocking collectives, shards(): lax.all_to_all(packed, 'dp', split_axis=0, concat_axis=0, tiled=True)  55.3 us
    all_to_all x1, starting transfers between devices, shards(): lax.all_to_all(back, 'dp', split_axis=0, concat_axis=0, tiled=True)  6.16 us
    all_to_all x1, waiting for transfers between devices, shards(): lax.all_to_all(back, 'dp', split_axis=0, concat_axis=0, tiled=True)  5.57 us
    ppermute x1, starting transfers between devices, shards(): other_c = lax.ppermute(sent_c, 'rep', [(0, 1), (1, 0)])  3.95 us
    pallas_call x1, Pallas kernels, shards(): pl.pallas_call(other_kernel, out_shape=(jax.ShapeDtypeStruct((PEERS, 128)...  3.69 us
    pallas_call x1, Pallas kernels, shards(): pl.pallas_call(pack_kernel, out_shape=pltpu.VMEM((PEERS, 48, HALF), BF16)...  3.28 us
    psum x1, blocking collectives, shards(): loss_total = lax.psum(loss_sum[0, 0], 'rep')  2.98 us
    pallas_call x1, Pallas kernels, shards(): pl.pallas_call(own_kernel, out_shape=(line, line, short), in_specs=[VMEM]...  2.92 us
  transfers between devices with their start and end apart: 2, of which 1 were waited for; matrix products, arithmetic and copies ran while one was open for 0% of the time, Pallas kernels for 5%

profile of v2, /device:TPU:1, one launch (start us, length us, event | category | flops | bytes accessed | tf_op | source)
XLA Modules:
  0.0 94.2 jit_solution(10662701702929537163)
XLA Ops:
  0.6 3.3 %pack.1 = bf16[128,48,128]{2,1,0:T(8,128)(2,1)S(1)} custom-call(s32[1,768]{1,0:T(1,128)} %bitcast.15, bf16[768,256]{1,0:T(8,128)(2,1)} %q_ref.3, bf16[768,256]{1,0:T(8,128)(2,1)} %c_ref.3), custom_call_target="tpu_custom_call" | custom-call | tf_op jit(solution)/shard_map/pack/pallas_call | solution.py:239
  3.9 55.3 %all_to_all.16.in_ref = bf16[128,48,128]{2,1,0:T(8,128)(2,1)S(1)} all-to-all(bf16[128,48,128]{2,1,0:T(8,128)(2,1)S(1)} %pack.1), channel_id=1, replica_groups=mesh['dp'=128,'rep'=2] {'dp'}, dimensions={0} | all-to-all | bytes 3145728 | tf_op jit(solution)/shard_map/all_to_all | solution.py:246
  59.2 1.4 %unpack.1 = (bf16[1536,256]{1,0:T(8,128)(2,1)S(1)}, bf16[1536,256]{1,0:T(8,128)(2,1)S(1)}, bf16[1536,256]{1,0:T(8,128)(2,1)}) custom-call(bf16[128,48,128]{2,1,0:T(8,128)(2,1)S(1)} %all_to_all.16.in_ref), custom_call_target="tpu_custom_call" | custom-call | tf_op jit(solution)/shard_map/unpack/pallas_call | solution.py:258
  60.6 0.0 copy-start
  60.6 0.9 copy-done
  61.5 3.9 %collective-permute-start = (bf16[1536,256]{1,0:T(8,128)(2,1)}, bf16[1536,256]{1,0:T(8,128)(2,1)S(1)}, u32[]{:S(2)}, u32[]{:S(2)}) collective-permute-start(bf16[1536,256]{1,0:T(8,128)(2,1)} %get-tuple-element.17), channel_id=1, source_target_pairs={{0,1},{1,0},{2,3},{3,2},{4,5},{5,4},{6,7},{7,6},{8,9},{9,8},{10,11... | collective-permute-start | bytes 2359304 | tf_op jit(solution)/shard_map/ppermute | solution.py:265
  65.5 0.0 copy-start.1
  65.5 1.1 %copy-done.1 = bf16[1536,256]{1,0:T(8,128)(2,1)S(1)} copy-done((bf16[1536,256]{1,0:T(8,128)(2,1)S(1)}, bf16[1536,256]{1,0:T(8,128)(2,1)}, u32[]{:S(2)}) %copy-start.1) | copy-done | bytes 786456
  66.6 2.9 %own.1 = (f32[1,1536]{1,0:T(1,128)S(1)}, f32[1,1536]{1,0:T(1,128)S(1)}, f32[1,128]{1,0:T(1,128)S(1)}) custom-call(bf16[1536,256]{1,0:T(8,128)(2,1)S(1)} %copy-done.1, bf16[1536,256]{1,0:T(8,128)(2,1)S(1)} %get-tuple-element.16.c_ref.own_ref), custom_call_target="tpu_custom_call" | custom-call | tf_op jit(solution)/shard_map/own/pallas_call | solution.py:269
  69.5 0.0 collective-permute-done.c_ref
  69.5 3.7 %other.1 = (f32[128,128]{1,0:T(8,128)}, f32[1,128]{1,0:T(1,128)S(1)}, f32[1,128]{1,0:T(1,128)S(1)}) custom-call(bf16[1536,256]{1,0:T(8,128)(2,1)S(1)} %copy-done.1, bf16[1536,256]{1,0:T(8,128)(2,1)S(1)} %get-tuple-element.16.c_ref.own_ref, bf16[1536,256]{1,0:T(8,128)(2,1)S(1)} %collective-permute-done.c_ref, f32[1,1536]{1,0:T(1,128)S(1)} %get-tuple-element.18.top_ref, ...), custom_call_target="tpu_custom_call" | custom-call | tf_op jit(solution)/shard_map/other/pallas_call | solution.py:277
  73.2 6.2 %all-to-all-start.1 = ((f32[128,1,128]{2,1,0:T(1,128)}), f32[128,1,128]{2,1,0:T(1,128)S(1)}, u32[]{:S(2)}, u32[]{:S(2)}) async-start(f32[128,1,128]{2,1,0:T(1,128)} %bitcast.14), calls=%async_computation.1 | async-start | bytes 131072 | tf_op jit(solution)/shard_map/all_to_all | solution.py:285
  79.4 1.6 %positive.1 = (f32[1,768]{1,0:T(1,128)S(1)}, s32[1,768]{1,0:T(1,128)S(1)}) custom-call(s32[1,768]{1,0:T(1,128)} %bitcast.16, bf16[768,256]{1,0:T(8,128)(2,1)} %q_ref.3, bf16[768,256]{1,0:T(8,128)(2,1)} %c_ref.3), custom_call_target="tpu_custom_call" | custom-call | tf_op jit(solution)/shard_map/positive/pallas_call | solution.py:247
  80.9 3.0 %psum.7 = f32[]{:T(128)} all-reduce(f32[]{:T(128)S(1)} %bitcast.13), channel_id=1, replica_groups=mesh['dp'=128,'rep'=2] {'rep'}, use_global_device_ids=true, to_apply=%region_0.0 | all-reduce | flops 1 | bytes 8 | tf_op jit(solution)/shard_map/psum | solution.py:286
  84.6 5.6 %all-to-all-done.1 = f32[128,1,128]{2,1,0:T(1,128)S(1)} async-done(((f32[128,1,128]{2,1,0:T(1,128)}), f32[128,1,128]{2,1,0:T(1,128)S(1)}, u32[]{:S(2)}, u32[]{:S(2)}) %all-to-all-start.1) | async-done | bytes 65568 | tf_op jit(solution)/shard_map/all_to_all | solution.py:285
  90.2 1.6 %finish.1 = f32[1,768]{1,0:T(1,128)} custom-call(s32[1]{0:T(128)} %bitcast.at_ref, s32[1,768]{1,0:T(1,128)} %bitcast.17, s32[1,768]{1,0:T(1,128)S(1)} %get-tuple-element.13.rank_ref, f32[1,768]{1,0:T(1,128)S(1)} %get-tuple-element.14.pos_ref, f32[128,128]{1,0:T(8,128)S(1)} %bitcast.11), custom_call_target="tpu_custom_call" | custom-call | tf_op jit(solution)/shard_map/finish/pallas_call | solution.py:289
  91.8 1.3 %reduce = f32[768]{0:T(1024)} reduce(f32[1,768]{1,0:T(1,128)} %finish.1, f32[]{:T(128)} %constant.6), dimensions={0}, to_apply=%pallas_call.45.reduce_sub_computation | reduce | bytes 6148 | tf_op jit(solution)/shard_map/finish/pallas_call | solution.py:289
Async XLA Ops:
  60.6 0.9 copy-start
  61.5 8.0 %collective-permute-start = (bf16[1536,256]{1,0:T(8,128)(2,1)}, bf16[1536,256]{1,0:T(8,128)(2,1)S(1)}, u32[]{:S(2)}, u32[]{:S(2)}) collective-permute-start(bf16[1536,256]{1,0:T(8,128)(2,1)} %get-tuple-element.17), channel_id=1, source_target_pairs={{0,1},{1,0},{2,3},{3,2},{4,5},{5,4},{6,7},{7,6},{8,9},{9,8},{10,11... | collective-permute-start | bytes 2359304 | tf_op jit(solution)/shard_map/ppermute | solution.py:265
  65.5 1.1 %copy-start.1 = (bf16[1536,256]{1,0:T(8,128)(2,1)S(1)}, bf16[1536,256]{1,0:T(8,128)(2,1)}, u32[]{:S(2)}) copy-start(bf16[1536,256]{1,0:T(8,128)(2,1)} %copy-done) | copy-start | bytes 2359300
  73.2 17.0 %all-to-all-start.1 = ((f32[128,1,128]{2,1,0:T(1,128)}), f32[128,1,128]{2,1,0:T(1,128)S(1)}, u32[]{:S(2)}, u32[]{:S(2)}) async-start(f32[128,1,128]{2,1,0:T(1,128)} %bitcast.14), calls=%async_computation.1 | async-start | bytes 131072 | tf_op jit(solution)/shard_map/all_to_all | solution.py:285

commit v3 on v1

v3 whole, which is shorter than its diff:
```python
import math

import jax
import jax.numpy as jnp
from jax import lax
from jax.experimental import pallas as pl
from jax.experimental.pallas import tpu as pltpu
from jax.sharding import PartitionSpec as P

ROWS = 768
WIDTH = 256
HALF = 128
PEERS = 128
CAP = 12
SLOTS = PEERS * CAP
MAIN = PEERS * 8
REST = PEERS * 4
ABSENT = 64.0
NEG = -1e30
LN2 = math.log(2.0)
TO_LOG2 = 0.0625 / LN2

F32 = jnp.float32
BF16 = jnp.bfloat16
VMEM = pl.BlockSpec(memory_space=pltpu.VMEM)


def iota(shape, dim):
    return lax.broadcasted_iota(jnp.int32, shape, dim)


def dot_nn(a, b):
    return lax.dot_general(a, b, (((1,), (0,)), ((), ())), preferred_element_type=F32)


def dot_nt(a, b):
    return lax.dot_general(a, b, (((1,), (1,)), ((), ())), preferred_element_type=F32)


def dot_tn(a, b):
    return lax.dot_general(a, b, (((0,), (0,)), ((), ())), preferred_element_type=F32)


def ranks(b):
    blocks = ROWS // 128
    row = iota((128, 128), 0)
    hot = [(row == b[:, j * 128 : (j + 1) * 128]).astype(F32) for j in range(blocks)]
    stack = jnp.concatenate(hot, axis=0).astype(BF16)
    upper = (iota((128, 256), 0) < iota((128, 256), 1)).astype(F32).astype(BF16)
    both = dot_nn(stack, upper)
    before = jnp.zeros((128, 128), F32)
    rank = []
    for j in range(blocks):
        at = both[j * 128 : (j + 1) * 128]
        rank.append(jnp.sum(hot[j] * (at[:, :128] + before), axis=0, keepdims=True))
        before = before + at[:, 128:]
    return jnp.concatenate(rank, axis=1).astype(jnp.int32), before


def pack_kernel(b_hbm, q_hbm, c_hbm, out_ref, b_ref, q_ref, c_ref, b_sem, q_sem, c_sem):
    load_b = pltpu.make_async_copy(b_hbm, b_ref, b_sem)
    load_c = pltpu.make_async_copy(c_hbm, c_ref, c_sem)
    load_q = pltpu.make_async_copy(q_hbm, q_ref, q_sem)
    load_b.start()
    load_c.start()
    load_q.start()
    load_b.wait()
    b = b_ref[...]
    rank, count = ranks(b)
    count = count.astype(jnp.int32)
    main_key = jnp.where(rank < 8, b * 8 + rank, -1)
    rest_key = jnp.where(rank >= 8, b * 8 + rank - 8, -1)
    step = 32
    load_c.wait()
    load_q.wait()
    q = q_ref[...]
    c = c_ref[...]
    for p0 in range(0, PEERS, step):
        n = step * 8
        ids = iota((n, ROWS), 0) + p0 * 8
        main = (ids == main_key).astype(F32).astype(BF16)
        rest = ((ids & ~4) == rest_key).astype(F32).astype(BF16)
        c_main = dot_nn(main, c).reshape(step, 8, WIDTH)
        q_main = dot_nn(main, q).reshape(step, 8, WIDTH)
        c_rest = dot_nn(rest, c).reshape(step, 8, WIDTH)
        q_rest = dot_nn(rest, q).reshape(step, 8, WIDTH)
        slot = iota((step, 8, HALF), 1)
        lane = iota((step, 8, HALF), 2)
        have = jnp.broadcast_to(count[p0 : p0 + step][:, None, :], (step, 8, HALF))
        c_lo = jnp.where((lane == 0) & (slot >= have), ABSENT, c_main[:, :, :HALF])
        r_lo = jnp.where(
            slot < 4,
            jnp.where((lane == 0) & (slot + 8 >= have), ABSENT, c_rest[:, :, :HALF]),
            q_rest[:, :, :HALF],
        )
        r_hi = jnp.where(slot < 4, c_rest[:, :, HALF:], q_rest[:, :, HALF:])
        out_ref[p0 : p0 + step, 0:16, :] = jnp.concatenate(
            [c_lo, c_main[:, :, HALF:]], axis=1
        ).astype(BF16)
        out_ref[p0 : p0 + step, 16:32, :] = jnp.concatenate([r_lo, r_hi], axis=1).astype(BF16)
        out_ref[p0 : p0 + step, 32:48, :] = jnp.concatenate(
            [q_main[:, :, :HALF], q_main[:, :, HALF:]], axis=1
        ).astype(BF16)


def main_rows(in_ref, at, ref):
    tile = in_ref[:, at : at + 16, :].astype(F32)
    ref[0:MAIN, :HALF] = tile[:, :8, :].reshape(MAIN, HALF).astype(BF16)
    ref[0:MAIN, HALF:] = tile[:, 8:, :].reshape(MAIN, HALF).astype(BF16)


def rest_rows(in_ref, second, ref):
    tile = in_ref[:, 16:32, :].astype(F32)
    first = iota((PEERS // 2, 8, HALF), 1) < 4
    for half in range(2):
        part = tile[:, half * 8 : half * 8 + 8, :].reshape(PEERS // 2, 2, 8, HALF)
        even = part[:, 0]
        odd = part[:, 1]
        if second:
            rows = jnp.where(first, pltpu.roll(even, 4, 1), odd)
        else:
            rows = jnp.where(first, even, pltpu.roll(odd, 4, 1))
        ref[MAIN:SLOTS, half * HALF : (half + 1) * HALF] = rows.reshape(REST, HALF).astype(BF16)


def candidates_kernel(in_ref, c_ref):
    main_rows(in_ref, 0, c_ref)
    rest_rows(in_ref, False, c_ref)


COLS = 256
CHUNK = 256


def scores_of(q_ref, c_ref, bias_ref, t_ref, done):
    count = jnp.zeros((1, 1), F32)
    for k in range(SLOTS // CHUNK):
        at = slice(k * CHUNK, (k + 1) * CHUNK)
        absent = c_ref[at, 0:1].astype(F32) == ABSENT
        bias_ref[at, :] = jnp.broadcast_to(jnp.where(absent, NEG, 0.0), (CHUNK, HALF))
        count = count + jnp.sum(jnp.where(absent, 0.0, 1.0), axis=0, keepdims=True)

    blocks = SLOTS // COLS
    top = total = None
    for j in range(blocks + 1):
        if j < blocks:
            q = q_ref[j * COLS : (j + 1) * COLS, :]
            new_top = jnp.full((8, COLS), NEG * 2, F32)
        if j > 0:
            total = jnp.zeros((8, COLS), F32)
        for k in range(SLOTS // CHUNK):
            at = slice(k * CHUNK, (k + 1) * CHUNK)
            if j < blocks:
                s = dot_nt(c_ref[at, :], q)
                bias = bias_ref[at, :]
                t = s * TO_LOG2 + jnp.concatenate([bias, bias], axis=1)
                t_ref[j % 2, at, :] = t
                new_top = jnp.maximum(new_top, jnp.max(t.reshape(CHUNK // 8, 8, COLS), axis=0))
            if j > 0:
                e = jnp.exp2(t_ref[(j - 1) % 2, at, :] - top)
                total = total + jnp.sum(e.reshape(CHUNK // 8, 8, COLS), axis=0)
        if j > 0:
            done(j - 1, top, jnp.sum(total, axis=0, keepdims=True))
        if j < blocks:
            top = jnp.max(new_top, axis=0, keepdims=True)
    return count


def own_kernel(in_ref, c_ref, q_ref, top_ref, total_ref, count_ref, bias_ref, t_ref):
    main_rows(in_ref, 32, q_ref)
    rest_rows(in_ref, True, q_ref)

    def done(j, top, total):
        top_ref[:, j * COLS : (j + 1) * COLS] = top
        total_ref[:, j * COLS : (j + 1) * COLS] = total

    count = scores_of(q_ref, c_ref, bias_ref, t_ref, done)
    count_ref[...] = jnp.broadcast_to(count, (1, 128))


def other_kernel(
    q_ref, c_ref, top_ref, total_ref, count_ref, out_ref, lse_ref, n_ref, bias_ref, t_ref
):
    def done(j, top, total):
        top0 = top_ref[:, j * COLS : (j + 1) * COLS]
        total0 = total_ref[:, j * COLS : (j + 1) * COLS]
        new = jnp.maximum(top0, top)
        both = total0 * jnp.exp2(top0 - new) + total * jnp.exp2(top - new)
        lse_ref[:, j * COLS : (j + 1) * COLS] = new * LN2 + jnp.log(both)

    count = scores_of(q_ref, c_ref, bias_ref, t_ref, done) + count_ref[:, 0:1]
    n = jnp.broadcast_to(count, (1, 128))
    n_ref[...] = n
    log_n = jnp.log(jnp.maximum(n, 1.0))
    lines = [lse_ref[:, t * 128 : (t + 1) * 128] - log_n for t in range(CAP)]
    for t in range(CAP):
        lse_ref[:, t * 128 : (t + 1) * 128] = lines[t]
    lane = iota((1, 128), 1)
    for u in range(PEERS // 8):
        a = lines[u // 2]
        if u % 2:
            a = pltpu.roll(a, 64, 1)
        r = lines[8 + u // 4]
        shift = (64 - 32 * (u % 4)) % 128
        if shift:
            r = pltpu.roll(r, shift, 1)
        line = jnp.where(lane < 64, a, jnp.where(lane < 96, r, 0.0))
        out_ref[u * 8 : (u + 1) * 8, :] = jnp.broadcast_to(line, (8, 128))


def sum_kernel(in_ref, lse_ref, n_ref, sum_ref):
    total = jnp.sum(lse_ref[...], axis=1, keepdims=True)
    total = jnp.where(n_ref[:, 0:1] > 0, total, 0.0)
    c = in_ref[:, 0:16, :].astype(F32)
    q = in_ref[:, 32:48, :].astype(F32)
    pos = jnp.sum(c * q, axis=0)
    z = in_ref[:, 16:32, :].astype(F32).reshape(PEERS * 2, 8, HALF)
    low = iota((PEERS * 2, 8, HALF), 1) < 4
    rest = jnp.sum(jnp.where(low, z * pltpu.roll(z, 4, 1), 0.0), axis=0)
    pos = jnp.sum(jnp.sum(pos, axis=0, keepdims=True), axis=1, keepdims=True)
    rest = jnp.sum(jnp.sum(rest, axis=0, keepdims=True), axis=1, keepdims=True)
    sum_ref[...] = jnp.broadcast_to(total - (pos + rest) * 0.0625, (1, 128))


def positive_kernel(at_ref, b_ref, q_ref, c_ref, pos_ref, hot_ref, lane_ref):
    rank, _ = ranks(b_ref[...])
    eighth = at_ref[0] & 7
    lane_ref[...] = jnp.where(rank < 8, eighth * 8 + rank, 64 + eighth * 4 + rank - 8)
    hot_ref[...] = (iota((PEERS, ROWS), 0) == b_ref[...]).astype(F32).astype(BF16)
    both = q_ref[...].astype(F32) * c_ref[...].astype(F32)
    hi = both.astype(BF16)
    lo = (both - hi.astype(F32)).astype(BF16)
    ones = jnp.ones((8, WIDTH), BF16)
    pos_ref[...] = ((dot_nt(ones, hi) + dot_nt(ones, lo)) * 0.0625)[0:1]


def finish_kernel(hot_ref, lane_ref, pos_ref, back_ref, out_ref):
    hot = hot_ref[...]
    x = back_ref[...]
    hi = x.astype(BF16)
    left = x - hi.astype(F32)
    mid = left.astype(BF16)
    lo = (left - mid.astype(F32)).astype(BF16)
    picked = (dot_tn(hi, hot) + dot_tn(mid, hot)) + dot_tn(lo, hot)
    mine = jnp.where(iota((128, ROWS), 0) == lane_ref[...], picked, 0.0)
    mine = jnp.sum(mine, axis=0, keepdims=True) - pos_ref[...]
    for j in range(ROWS // 128):
        out_ref[j : j + 1, :] = mine[:, j * 128 : (j + 1) * 128]


def call(kernel, name, out_shape, *args, specs=None, scratch=()):
    single = not isinstance(out_shape, tuple)
    return pl.pallas_call(
        kernel,
        out_shape=out_shape,
        in_specs=specs or [VMEM] * len(args),
        out_specs=VMEM if single else (VMEM,) * len(out_shape),
        scratch_shapes=scratch,
        compiler_params=pltpu.CompilerParams(vmem_limit_bytes=24 * 1024 * 1024),
        name=name,
    )(*args)


def exchange(x):
    return lax.all_to_all(x, "dp", split_axis=0, concat_axis=0, tiled=True)


def shards(queries, candidates, bucket):
    b = bucket.reshape(1, ROWS)
    me = lax.axis_index("dp").astype(jnp.int32).reshape(1)
    shape = jax.ShapeDtypeStruct
    hbm = pl.BlockSpec(memory_space=pltpu.HBM)
    rows = pltpu.VMEM((ROWS, WIDTH), BF16)
    packed = call(
        pack_kernel, "pack", shape((PEERS, 48, HALF), BF16),
        *[pltpu.with_memory_space_constraint(x, pltpu.HBM) for x in (b, queries, candidates)],
        specs=[hbm] * 3,
        scratch=[pltpu.VMEM((1, ROWS), jnp.int32), rows, rows] + [pltpu.SemaphoreType.DMA] * 3,
    )
    received = exchange(packed)
    own_c = call(candidates_kernel, "candidates", shape((SLOTS, WIDTH), BF16), received)
    other_c = lax.ppermute(own_c, "rep", [(0, 1), (1, 0)])
    line = shape((1, SLOTS), F32)
    short = shape((1, 128), F32)
    scratch = [pltpu.VMEM((SLOTS, HALF), F32), pltpu.VMEM((2, SLOTS, COLS), F32)]
    own_q, top, total, count = call(
        own_kernel, "own", (shape((SLOTS, WIDTH), BF16), line, line, short),
        received, own_c, scratch=scratch,
    )
    back, lse, n = call(
        other_kernel, "other", (shape((PEERS, 128), F32), line, short),
        own_q, other_c, top, total, count, scratch=scratch,
    )
    returned = exchange(back)
    pos, hot, lane = call(
        positive_kernel, "positive",
        (shape((1, ROWS), F32), shape((PEERS, ROWS), BF16), shape((1, ROWS), jnp.int32)),
        me, b, queries, candidates, specs=[pl.BlockSpec(memory_space=pltpu.SMEM)] + [VMEM] * 3,
    )
    loss_sum = call(sum_kernel, "sum", short, received, lse, n)
    loss_total = lax.psum(loss_sum[0, 0], "rep")
    bucket_loss = (loss_total / jnp.maximum(n[0, 0], 1.0)).reshape(1)
    query_loss = call(
        finish_kernel, "finish", shape((ROWS // 128, 128), F32), hot, lane, pos, returned
    )
    return (query_loss.reshape(ROWS), bucket_loss)


def solution(mesh):
    in_specs = (P(("dp", "rep"), None), P(("dp", "rep"), None), P(("dp", "rep"), None))
    out_specs = (P(("dp", "rep")), P("dp"))
    return jax.shard_map(shards, mesh=mesh, in_specs=in_specs, out_specs=out_specs, check_vma=False)
```

time: 101 us -> 89.4 us (0.89)
  Pallas kernels: 21.4 us -> 12 us
  waiting for transfers between devices: 4.22 us -> 6.11 us
  local copies, waits for them, and re-layouts: 1.51 us -> 0.02 us
  other arithmetic: 1.29 us -> 0 us
    pallas_call x6 -> x7, Pallas kernels: 21.4 us -> 12 us  [call(): pl.pallas_call(kernel, out_shape=out_shape, in_specs=specs or [VMEM] * le...]
    all_to_all x1, waiting for transfers between devices: 4.22 us -> 6.1 us  [exchange(): return lax.all_to_all(x, 'dp', split_axis=0, concat_axis=0, tiled=True)]
    unnamed x4 -> x6, local copies, waits for them, and re-layouts: 1.51 us -> 0.02 us
    pallas_call x1 -> x0, other arithmetic: 1.29 us -> none  [shards(): pl.pallas_call(finish_kernel, out_shape=jax.ShapeDtypeStruct((1, ROWS), F...]
  transfers between devices with their start and end apart: 2 -> 2, of which waited for: 1 -> 1; matrix products, arithmetic and copies ran while one was open for 0% -> 0% of each run, Pallas kernels for 7% -> 5%
where the time goes in v3:
time: 89.4 us; the launch traced here: 89.1 us
  blocking collectives  58.3 us (65%)
  Pallas kernels  12 us (13%)
  starting transfers between devices  10.2 us (11%)
  waiting for transfers between devices  6.11 us (7%)
  between operations  2.54 us (3%)
    all_to_all x1, blocking collectives, exchange(): return lax.all_to_all(x, 'dp', split_axis=0, concat_axis=0, tiled=True)  55.3 us
    pallas_call x7, Pallas kernels, call(): pl.pallas_call(kernel, out_shape=out_shape, in_specs=specs or [VMEM] * le...  12 us
    all_to_all x1, starting transfers between devices, exchange(): return lax.all_to_all(x, 'dp', split_axis=0, concat_axis=0, tiled=True)  6.18 us
    all_to_all x1, waiting for transfers between devices, exchange(): return lax.all_to_all(x, 'dp', split_axis=0, concat_axis=0, tiled=True)  6.1 us
    ppermute x1, starting transfers between devices, shards(): other_c = lax.ppermute(own_c, 'rep', [(0, 1), (1, 0)])  4.06 us
    psum x1, blocking collectives, shards(): loss_total = lax.psum(loss_sum[0, 0], 'rep')  2.96 us
  transfers between devices with their start and end apart: 2, of which 1 were waited for; matrix products, arithmetic and copies ran while one was open for 0% of the time, Pallas kernels for 5%

profile of v3, /device:TPU:1, one launch (start us, length us, event | category | flops | bytes accessed | tf_op | source)
XLA Modules:
  0.0 89.1 jit_solution(7492706901254703038)
XLA Ops:
  0.6 3.0 %pack.1 = bf16[128,48,128]{2,1,0:T(8,128)(2,1)S(1)} custom-call(s32[1,768]{1,0:T(1,128)} %bitcast.13, bf16[768,256]{1,0:T(8,128)(2,1)} %q_hbm.1, bf16[768,256]{1,0:T(8,128)(2,1)} %c_hbm.1), custom_call_target="tpu_custom_call" | custom-call | tf_op jit(solution)/shard_map/pack/pallas_call | solution.py:253
  3.6 55.3 %all_to_all.16.in_ref = bf16[128,48,128]{2,1,0:T(8,128)(2,1)S(1)} all-to-all(bf16[128,48,128]{2,1,0:T(8,128)(2,1)S(1)} %pack.1), channel_id=1, replica_groups=mesh['dp'=128,'rep'=2] {'dp'}, dimensions={0} | all-to-all | bytes 3145728 | tf_op jit(solution)/shard_map/all_to_all | solution.py:265
  58.9 0.2 candidates.1.c_ref
  59.1 0.0 copy-start
  59.1 0.0 copy-start.1
  59.1 0.0 copy-start.2
  59.1 4.1 %collective-permute-start = (bf16[1536,256]{1,0:T(8,128)(2,1)S(1)}, bf16[1536,256]{1,0:T(8,128)(2,1)S(1)}, u32[]{:S(2)}, u32[]{:S(2)}) collective-permute-start(bf16[1536,256]{1,0:T(8,128)(2,1)S(1)} %candidates.1.c_ref), channel_id=1, source_target_pairs={{0,1},{1,0},{2,3},{3,2},{4,5},{5,4},{6,7},{7,6},{8,9},{9,8},{10,11... | collective-permute-start | bytes 2359304 | tf_op jit(solution)/shard_map/ppermute | solution.py:282
  63.2 3.1 %own.1 = (bf16[1536,256]{1,0:T(8,128)(2,1)S(1)}, f32[1,1536]{1,0:T(1,128)S(1)}, f32[1,1536]{1,0:T(1,128)S(1)}, f32[1,128]{1,0:T(1,128)S(1)}) custom-call(bf16[128,48,128]{2,1,0:T(8,128)(2,1)S(1)} %all_to_all.16.in_ref, bf16[1536,256]{1,0:T(8,128)(2,1)S(1)} %candidates.1.c_ref), custom_call_target="tpu_custom_call" | custom-call | tf_op jit(solution)/shard_map/own/pallas_call | solution.py:253
  66.3 0.0 collective-permute-done.c_ref
  66.3 3.8 %other.1 = (f32[128,128]{1,0:T(8,128)}, f32[1,1536]{1,0:T(1,128)S(1)}, f32[1,128]{1,0:T(1,128)S(1)}) custom-call(bf16[1536,256]{1,0:T(8,128)(2,1)S(1)} %get-tuple-element.15.q_ref, bf16[1536,256]{1,0:T(8,128)(2,1)S(1)} %collective-permute-done.c_ref, f32[1,1536]{1,0:T(1,128)S(1)} %get-tuple-element.16.top_ref, f32[1,1536]{1,0:T(1,128)S(1)} %get-tuple-element.17.total_ref, ...), custom_call_target="tpu_custom_call" | custom-call | tf_op jit(solution)/shard_map/other/pallas_call | solution.py:253
  70.1 6.2 %all-to-all-start.1 = ((f32[128,1,128]{2,1,0:T(1,128)}), f32[128,1,128]{2,1,0:T(1,128)S(1)}, u32[]{:S(2)}, u32[]{:S(2)}) async-start(f32[128,1,128]{2,1,0:T(1,128)} %bitcast.3), calls=%async_computation.1 | async-start | bytes 131072 | tf_op jit(solution)/shard_map/all_to_all | solution.py:265
  76.3 0.0 copy-done
  76.3 0.0 copy-done.1
  76.3 0.0 copy-done.2
  76.3 0.5 positive.1
  76.8 0.5 sum.1
  77.3 3.0 %psum.7 = f32[]{:T(128)} all-reduce(f32[]{:T(128)S(1)} %bitcast.16), channel_id=1, replica_groups=mesh['dp'=128,'rep'=2] {'rep'}, use_global_device_ids=true, to_apply=%region_0.0 | all-reduce | flops 1 | bytes 8 | tf_op jit(solution)/shard_map/psum | solution.py:301
  80.9 6.1 %all-to-all-done.1 = f32[128,1,128]{2,1,0:T(1,128)S(1)} async-done(((f32[128,1,128]{2,1,0:T(1,128)}), f32[128,1,128]{2,1,0:T(1,128)S(1)}, u32[]{:S(2)}, u32[]{:S(2)}) %all-to-all-start.1) | async-done | bytes 65568 | tf_op jit(solution)/shard_map/all_to_all | solution.py:265
  87.0 1.0 %finish.1 = f32[6,128]{1,0:T(8,128)} custom-call(bf16[128,768]{1,0:T(8,128)(2,1)S(1)} %get-tuple-element.12.hot_ref, s32[1,768]{1,0:T(1,128)S(1)} %get-tuple-element.13.lane_ref, f32[1,768]{1,0:T(1,128)S(1)} %get-tuple-element.14.pos_ref, f32[128,128]{1,0:T(8,128)S(1)} %bitcast.12), custom_call_target="tpu_custom_call" | custom-call | tf_op jit(solution)/shard_map/finish/pallas_call | solution.py:253
Async XLA Ops:
  59.1 17.2 %copy-start = (bf16[768,256]{1,0:T(8,128)(2,1)S(1)}, bf16[768,256]{1,0:T(8,128)(2,1)}, u32[]{:S(2)}) copy-start(bf16[768,256]{1,0:T(8,128)(2,1)} %q_hbm.1) | copy-start | bytes 1179652
  59.1 17.2 %copy-start.1 = (bf16[768,256]{1,0:T(8,128)(2,1)S(1)}, bf16[768,256]{1,0:T(8,128)(2,1)}, u32[]{:S(2)}) copy-start(bf16[768,256]{1,0:T(8,128)(2,1)} %c_hbm.1) | copy-start | bytes 1179652
  59.1 17.2 %copy-start.2 = (s32[768,1]{0,1:T(1,128)S(1)}, s32[768,1]{0,1:T(1,128)}, u32[]{:S(2)}) copy-start(s32[768,1]{0,1:T(1,128)} %param.5) | copy-start | bytes 9220
  59.1 7.2 %collective-permute-start = (bf16[1536,256]{1,0:T(8,128)(2,1)S(1)}, bf16[1536,256]{1,0:T(8,128)(2,1)S(1)}, u32[]{:S(2)}, u32[]{:S(2)}) collective-permute-start(bf16[1536,256]{1,0:T(8,128)(2,1)S(1)} %candidates.1.c_ref), channel_id=1, source_target_pairs={{0,1},{1,0},{2,3},{3,2},{4,5},{5,4},{6,7},{7,6},{8,9},{9,8},{10,11... | collective-permute-start | bytes 2359304 | tf_op jit(solution)/shard_map/ppermute | solution.py:282
  70.1 17.0 %all-to-all-start.1 = ((f32[128,1,128]{2,1,0:T(1,128)}), f32[128,1,128]{2,1,0:T(1,128)S(1)}, u32[]{:S(2)}, u32[]{:S(2)}) async-start(f32[128,1,128]{2,1,0:T(1,128)} %bitcast.3), calls=%async_computation.1 | async-start | bytes 131072 | tf_op jit(solution)/shard_map/all_to_all | solution.py:265

commit v4 on v3

--- a/solution.py
+++ b/solution.py
@@ -17,6 +17,7 @@
 REST = PEERS * 4
 ABSENT = 64.0
 NEG = -1e30
+HUGE = 1e37
 LN2 = math.log(2.0)
 TO_LOG2 = 0.0625 / LN2
 
@@ -69,35 +70,38 @@
     rank, count = ranks(b)
     count = count.astype(jnp.int32)
     main_key = jnp.where(rank < 8, b * 8 + rank, -1)
-    rest_key = jnp.where(rank >= 8, b * 8 + rank - 8, -1)
-    step = 32
+    rest_key = jnp.where(rank >= 8, b * 4 + rank - 8, -1)
+    step = 64
+    low = iota((step // 2, 8, WIDTH), 1) < 4
+    slot = iota((step, 8, HALF), 1)
+    lane = iota((step, 8, HALF), 2)
     load_c.wait()
     load_q.wait()
     q = q_ref[...]
     c = c_ref[...]
     for p0 in range(0, PEERS, step):
-        n = step * 8
-        ids = iota((n, ROWS), 0) + p0 * 8
-        main = (ids == main_key).astype(F32).astype(BF16)
-        rest = ((ids & ~4) == rest_key).astype(F32).astype(BF16)
-        c_main = dot_nn(main, c).reshape(step, 8, WIDTH)
-        q_main = dot_nn(main, q).reshape(step, 8, WIDTH)
-        c_rest = dot_nn(rest, c).reshape(step, 8, WIDTH)
-        q_rest = dot_nn(rest, q).reshape(step, 8, WIDTH)
-        slot = iota((step, 8, HALF), 1)
-        lane = iota((step, 8, HALF), 2)
+        main = (iota((step * 8, ROWS), 0) + p0 * 8 == main_key).astype(F32).astype(BF16)
+        rest = (iota((step * 4, ROWS), 0) + p0 * 4 == rest_key).astype(F32).astype(BF16)
+        both = jnp.concatenate([main, rest], axis=0)
+        c_both = dot_nn(both, c)
+        q_both = dot_nn(both, q)
+        c_main = c_both[: step * 8].reshape(step, 8, WIDTH)
+        q_main = q_both[: step * 8].reshape(step, 8, WIDTH)
+        c_rest = c_both[step * 8 :].reshape(step // 2, 8, WIDTH)
+        q_rest = q_both[step * 8 :].reshape(step // 2, 8, WIDTH)
+        even = jnp.where(low, c_rest, pltpu.roll(q_rest, 4, 1))
+        odd = jnp.where(low, pltpu.roll(c_rest, 4, 1), q_rest)
+        mixed = jnp.stack([even, odd], axis=1).reshape(step, 8, WIDTH)
         have = jnp.broadcast_to(count[p0 : p0 + step][:, None, :], (step, 8, HALF))
         c_lo = jnp.where((lane == 0) & (slot >= have), ABSENT, c_main[:, :, :HALF])
-        r_lo = jnp.where(
-            slot < 4,
-            jnp.where((lane == 0) & (slot + 8 >= have), ABSENT, c_rest[:, :, :HALF]),
-            q_rest[:, :, :HALF],
-        )
-        r_hi = jnp.where(slot < 4, c_rest[:, :, HALF:], q_rest[:, :, HALF:])
+        gone = (lane == 0) & (slot < 4) & (slot + 8 >= have)
+        r_lo = jnp.where(gone, ABSENT, mixed[:, :, :HALF])
         out_ref[p0 : p0 + step, 0:16, :] = jnp.concatenate(
             [c_lo, c_main[:, :, HALF:]], axis=1
         ).astype(BF16)
-        out_ref[p0 : p0 + step, 16:32, :] = jnp.concatenate([r_lo, r_hi], axis=1).astype(BF16)
+        out_ref[p0 : p0 + step, 16:32, :] = jnp.concatenate(
+            [r_lo, mixed[:, :, HALF:]], axis=1
+        ).astype(BF16)
         out_ref[p0 : p0 + step, 32:48, :] = jnp.concatenate(
             [q_main[:, :, :HALF], q_main[:, :, HALF:]], axis=1
         ).astype(BF16)
@@ -132,63 +136,118 @@
 CHUNK = 256
 
 
-def scores_of(q_ref, c_ref, bias_ref, t_ref, done):
+def fill_bias(c_ref, bias_ref):
     count = jnp.zeros((1, 1), F32)
     for k in range(SLOTS // CHUNK):
         at = slice(k * CHUNK, (k + 1) * CHUNK)
         absent = c_ref[at, 0:1].astype(F32) == ABSENT
         bias_ref[at, :] = jnp.broadcast_to(jnp.where(absent, NEG, 0.0), (CHUNK, HALF))
         count = count + jnp.sum(jnp.where(absent, 0.0, 1.0), axis=0, keepdims=True)
-
-    blocks = SLOTS // COLS
-    top = total = None
-    for j in range(blocks + 1):
-        if j < blocks:
-            q = q_ref[j * COLS : (j + 1) * COLS, :]
-            new_top = jnp.full((8, COLS), NEG * 2, F32)
-        if j > 0:
-            total = jnp.zeros((8, COLS), F32)
-        for k in range(SLOTS // CHUNK):
-            at = slice(k * CHUNK, (k + 1) * CHUNK)
-            if j < blocks:
-                s = dot_nt(c_ref[at, :], q)
-                bias = bias_ref[at, :]
-                t = s * TO_LOG2 + jnp.concatenate([bias, bias], axis=1)
-                t_ref[j % 2, at, :] = t
-                new_top = jnp.maximum(new_top, jnp.max(t.reshape(CHUNK // 8, 8, COLS), axis=0))
-            if j > 0:
-                e = jnp.exp2(t_ref[(j - 1) % 2, at, :] - top)
-                total = total + jnp.sum(e.reshape(CHUNK // 8, 8, COLS), axis=0)
-        if j > 0:
-            done(j - 1, top, jnp.sum(total, axis=0, keepdims=True))
-        if j < blocks:
-            top = jnp.max(new_top, axis=0, keepdims=True)
     return count
+
+
+def log2_scores(q, c_ref, bias_ref, at):
+    bias = bias_ref[at, :]
+    return dot_nt(c_ref[at, :], q) * TO_LOG2 + jnp.concatenate([bias, bias], axis=1)
+
+
+def eights(x, op):
+    return op(x.reshape(x.shape[0] // 8, 8, x.shape[1]), axis=0)
+
+
+def sums(q, c_ref, bias_ref, top, first):
+    total = jnp.zeros((8, COLS), F32)
+    for at in range(first, SLOTS, CHUNK):
+        t = log2_scores(q, c_ref, bias_ref, slice(at, at + CHUNK))
+        total = total + eights(jnp.exp2(t - top), jnp.sum)
+    return jnp.sum(total, axis=0, keepdims=True)
+
+
+def exact(q_ref, c_ref, bias_ref, t_ref, done):
+    def block(j, _):
+        cols = pl.ds(pl.multiple_of(j * COLS, COLS), COLS)
+        q = q_ref[cols, :]
+
+        def scores(k, top):
+            at = pl.ds(pl.multiple_of(k * CHUNK, CHUNK), CHUNK)
+            t = log2_scores(q, c_ref, bias_ref, at)
+            t_ref[at, :] = t
+            return jnp.maximum(top, eights(t, jnp.max))
+
+        top = lax.fori_loop(0, SLOTS // CHUNK, scores, jnp.full((8, COLS), 2 * NEG, F32))
+        top = jnp.max(top, axis=0, keepdims=True)
+
+        def add(k, total):
+            at = pl.ds(pl.multiple_of(k * CHUNK, CHUNK), CHUNK)
+            return total + eights(jnp.exp2(t_ref[at, :] - top), jnp.sum)
+
+        total = lax.fori_loop(0, SLOTS // CHUNK, add, jnp.zeros((8, COLS), F32))
+        done(cols, top, jnp.sum(total, axis=0, keepdims=True))
+        return 0
+
+    lax.fori_loop(0, SLOTS // COLS, block, 0)
+
+
+def too_large(totals):
+    worst = totals[0]
+    for total in totals[1:]:
+        worst = jnp.maximum(worst, total)
+    return jnp.max(worst) > HUGE
 
 
 def own_kernel(in_ref, c_ref, q_ref, top_ref, total_ref, count_ref, bias_ref, t_ref):
     main_rows(in_ref, 32, q_ref)
     rest_rows(in_ref, True, q_ref)
-
-    def done(j, top, total):
-        top_ref[:, j * COLS : (j + 1) * COLS] = top
-        total_ref[:, j * COLS : (j + 1) * COLS] = total
-
-    count = scores_of(q_ref, c_ref, bias_ref, t_ref, done)
-    count_ref[...] = jnp.broadcast_to(count, (1, 128))
+    count_ref[...] = jnp.broadcast_to(fill_bias(c_ref, bias_ref), (1, 128))
+    totals = []
+    top = None
+    for j in range(SLOTS // COLS + 1):
+        if j < SLOTS // COLS:
+            kept = slice((j % 2) * CHUNK, (j % 2 + 1) * CHUNK)
+            t = log2_scores(q_ref[j * COLS : (j + 1) * COLS, :], c_ref, bias_ref, slice(0, CHUNK))
+            t_ref[kept, :] = t
+            next_top = jnp.max(eights(t, jnp.max), axis=0, keepdims=True)
+        if j > 0:
+            cols = slice((j - 1) * COLS, j * COLS)
+            kept = slice(((j - 1) % 2) * CHUNK, ((j - 1) % 2 + 1) * CHUNK)
+            total = jnp.sum(eights(jnp.exp2(t_ref[kept, :] - top), jnp.sum), axis=0, keepdims=True)
+            total = total + sums(q_ref[cols, :], c_ref, bias_ref, top, CHUNK)
+            top_ref[:, cols] = top
+            total_ref[:, cols] = total
+            totals.append(total)
+        top = next_top
+
+    @pl.when(too_large(totals))
+    def _():
+        def done(cols, top, total):
+            top_ref[:, cols] = top
+            total_ref[:, cols] = total
+
+        exact(q_ref, c_ref, bias_ref, t_ref, done)
 
 
 def other_kernel(
     q_ref, c_ref, top_ref, total_ref, count_ref, out_ref, lse_ref, n_ref, bias_ref, t_ref
 ):
-    def done(j, top, total):
-        top0 = top_ref[:, j * COLS : (j + 1) * COLS]
-        total0 = total_ref[:, j * COLS : (j + 1) * COLS]
-        new = jnp.maximum(top0, top)
-        both = total0 * jnp.exp2(top0 - new) + total * jnp.exp2(top - new)
-        lse_ref[:, j * COLS : (j + 1) * COLS] = new * LN2 + jnp.log(both)
-
-    count = scores_of(q_ref, c_ref, bias_ref, t_ref, done) + count_ref[:, 0:1]
+    count = fill_bias(c_ref, bias_ref) + count_ref[:, 0:1]
+    totals = []
+    for j in range(SLOTS // COLS):
+        cols = slice(j * COLS, (j + 1) * COLS)
+        top = top_ref[:, cols]
+        total = sums(q_ref[cols, :], c_ref, bias_ref, top, 0)
+        lse_ref[:, cols] = top * LN2 + jnp.log(total_ref[:, cols] + total)
+        totals.append(total)
+
+    @pl.when(too_large(totals))
+    def _():
+        def done(cols, top, total):
+            top0 = top_ref[:, cols]
+            new = jnp.maximum(top0, top)
+            both = total_ref[:, cols] * jnp.exp2(top0 - new) + total * jnp.exp2(top - new)
+            lse_ref[:, cols] = new * LN2 + jnp.log(both)
+
+        exact(q_ref, c_ref, bias_ref, t_ref, done)
+
     n = jnp.broadcast_to(count, (1, 128))
     n_ref[...] = n
     log_n = jnp.log(jnp.maximum(n, 1.0))
@@ -282,7 +341,7 @@
     other_c = lax.ppermute(own_c, "rep", [(0, 1), (1, 0)])
     line = shape((1, SLOTS), F32)
     short = shape((1, 128), F32)
-    scratch = [pltpu.VMEM((SLOTS, HALF), F32), pltpu.VMEM((2, SLOTS, COLS), F32)]
+    scratch = [pltpu.VMEM((SLOTS, HALF), F32), pltpu.VMEM((SLOTS, COLS), F32)]
     own_q, top, total, count = call(
         own_kernel, "own", (shape((SLOTS, WIDTH), BF16), line, line, short),
         received, own_c, scratch=scratch,

time: 89.4 us -> 97.3 us (1.088)
  Pallas kernels: 12 us -> 19.9 us
    pallas_call x7, Pallas kernels: 12 us -> 19.9 us  [call(): pl.pallas_call(kernel, out_shape=out_shape, in_specs=specs or [VMEM] * le...]
  transfers between devices with their start and end apart: 2 -> 2, of which waited for: 1 -> 1; matrix products, arithmetic and copies ran while one was open for 0% -> 0% of each run, Pallas kernels for 5% -> 14%
where the time goes in v4:
time: 97.3 us; the launch traced here: 97.1 us
  blocking collectives  58.3 us (60%)
  Pallas kernels  19.9 us (20%)
  starting transfers between devices  10.2 us (10%)
  waiting for transfers between devices  6.12 us (6%)
  between operations  2.55 us (3%)
    all_to_all x1, blocking collectives, exchange(): return lax.all_to_all(x, 'dp', split_axis=0, concat_axis=0, tiled=True)  55.3 us
    pallas_call x7, Pallas kernels, call(): pl.pallas_call(kernel, out_shape=out_shape, in_specs=specs or [VMEM] * le...  19.9 us
    all_to_all x1, starting transfers between devices, exchange(): return lax.all_to_all(x, 'dp', split_axis=0, concat_axis=0, tiled=True)  6.18 us
    all_to_all x1, waiting for transfers between devices, exchange(): return lax.all_to_all(x, 'dp', split_axis=0, concat_axis=0, tiled=True)  6.12 us
    ppermute x1, starting transfers between devices, shards(): other_c = lax.ppermute(own_c, 'rep', [(0, 1), (1, 0)])  4.03 us
    psum x1, blocking collectives, shards(): loss_total = lax.psum(loss_sum[0, 0], 'rep')  2.96 us
  transfers between devices with their start and end apart: 2, of which 1 were waited for; matrix products, arithmetic and copies ran while one was open for 0% of the time, Pallas kernels for 14%

profile of v4, /device:TPU:1, one launch (start us, length us, event | category | flops | bytes accessed | tf_op | source)
XLA Modules:
  0.0 97.1 jit_solution(3117425844195091395)
XLA Ops:
  0.6 2.6 %pack.1 = bf16[128,48,128]{2,1,0:T(8,128)(2,1)S(1)} custom-call(s32[1,768]{1,0:T(1,128)} %bitcast.13, bf16[768,256]{1,0:T(8,128)(2,1)} %q_hbm.1, bf16[768,256]{1,0:T(8,128)(2,1)} %c_hbm.1), custom_call_target="tpu_custom_call" | custom-call | tf_op jit(solution)/shard_map/pack/pallas_call | solution.py:312
  3.2 55.3 %all_to_all.16.in_ref = bf16[128,48,128]{2,1,0:T(8,128)(2,1)S(1)} all-to-all(bf16[128,48,128]{2,1,0:T(8,128)(2,1)S(1)} %pack.1), channel_id=1, replica_groups=mesh['dp'=128,'rep'=2] {'dp'}, dimensions={0} | all-to-all | bytes 3145728 | tf_op jit(solution)/shard_map/all_to_all | solution.py:324
  58.5 0.2 candidates.1.c_ref
  58.7 0.0 copy-start
  58.7 0.0 copy-start.1
  58.7 0.0 copy-start.2
  58.8 4.0 %collective-permute-start = (bf16[1536,256]{1,0:T(8,128)(2,1)S(1)}, bf16[1536,256]{1,0:T(8,128)(2,1)S(1)}, u32[]{:S(2)}, u32[]{:S(2)}) collective-permute-start(bf16[1536,256]{1,0:T(8,128)(2,1)S(1)} %candidates.1.c_ref), channel_id=1, source_target_pairs={{0,1},{1,0},{2,3},{3,2},{4,5},{5,4},{6,7},{7,6},{8,9},{9,8},{10,11... | collective-permute-start | bytes 2359304 | tf_op jit(solution)/shard_map/ppermute | solution.py:341
  62.8 12.4 %own.1 = (bf16[1536,256]{1,0:T(8,128)(2,1)S(1)}, f32[1,1536]{1,0:T(1,128)S(1)}, f32[1,1536]{1,0:T(1,128)S(1)}, f32[1,128]{1,0:T(1,128)S(1)}) custom-call(bf16[128,48,128]{2,1,0:T(8,128)(2,1)S(1)} %all_to_all.16.in_ref, bf16[1536,256]{1,0:T(8,128)(2,1)S(1)} %candidates.1.c_ref), custom_call_target="tpu_custom_call" | custom-call | tf_op jit(solution)/shard_map/own/pallas_call | solution.py:312
  75.1 0.0 collective-permute-done.c_ref
  75.2 2.9 %other.1 = (f32[128,128]{1,0:T(8,128)}, f32[1,1536]{1,0:T(1,128)S(1)}, f32[1,128]{1,0:T(1,128)S(1)}) custom-call(bf16[1536,256]{1,0:T(8,128)(2,1)S(1)} %get-tuple-element.15.q_ref, bf16[1536,256]{1,0:T(8,128)(2,1)S(1)} %collective-permute-done.c_ref, f32[1,1536]{1,0:T(1,128)S(1)} %get-tuple-element.16.top_ref, f32[1,1536]{1,0:T(1,128)S(1)} %get-tuple-element.17.total_ref, ...), custom_call_target="tpu_custom_call" | custom-call | tf_op jit(solution)/shard_map/other/pallas_call | solution.py:312
  78.0 6.2 %all-to-all-start.1 = ((f32[128,1,128]{2,1,0:T(1,128)}), f32[128,1,128]{2,1,0:T(1,128)S(1)}, u32[]{:S(2)}, u32[]{:S(2)}) async-start(f32[128,1,128]{2,1,0:T(1,128)} %bitcast.3), calls=%async_computation.1 | async-start | bytes 131072 | tf_op jit(solution)/shard_map/all_to_all | solution.py:324
  84.2 0.0 copy-done
  84.2 0.0 copy-done.1
  84.2 0.0 copy-done.2
  84.3 0.5 positive.1
  84.7 0.5 sum.1
  85.2 3.0 %psum.7 = f32[]{:T(128)} all-reduce(f32[]{:T(128)S(1)} %bitcast.16), channel_id=1, replica_groups=mesh['dp'=128,'rep'=2] {'rep'}, use_global_device_ids=true, to_apply=%region_0.0 | all-reduce | flops 1 | bytes 8 | tf_op jit(solution)/shard_map/psum | solution.py:360
  88.9 6.1 %all-to-all-done.1 = f32[128,1,128]{2,1,0:T(1,128)S(1)} async-done(((f32[128,1,128]{2,1,0:T(1,128)}), f32[128,1,128]{2,1,0:T(1,128)S(1)}, u32[]{:S(2)}, u32[]{:S(2)}) %all-to-all-start.1) | async-done | bytes 65568 | tf_op jit(solution)/shard_map/all_to_all | solution.py:324
  95.0 1.0 finish.1
Async XLA Ops:
  58.7 25.5 %copy-start = (bf16[768,256]{1,0:T(8,128)(2,1)S(1)}, bf16[768,256]{1,0:T(8,128)(2,1)}, u32[]{:S(2)}) copy-start(bf16[768,256]{1,0:T(8,128)(2,1)} %q_hbm.1) | copy-start | bytes 1179652
  58.7 25.5 %copy-start.1 = (bf16[768,256]{1,0:T(8,128)(2,1)S(1)}, bf16[768,256]{1,0:T(8,128)(2,1)}, u32[]{:S(2)}) copy-start(bf16[768,256]{1,0:T(8,128)(2,1)} %c_hbm.1) | copy-start | bytes 1179652
  58.7 25.5 %copy-start.2 = (s32[768,1]{0,1:T(1,128)S(1)}, s32[768,1]{0,1:T(1,128)}, u32[]{:S(2)}) copy-start(s32[768,1]{0,1:T(1,128)} %param.5) | copy-start | bytes 9220
  58.8 16.4 %collective-permute-start = (bf16[1536,256]{1,0:T(8,128)(2,1)S(1)}, bf16[1536,256]{1,0:T(8,128)(2,1)S(1)}, u32[]{:S(2)}, u32[]{:S(2)}) collective-permute-start(bf16[1536,256]{1,0:T(8,128)(2,1)S(1)} %candidates.1.c_ref), channel_id=1, source_target_pairs={{0,1},{1,0},{2,3},{3,2},{4,5},{5,4},{6,7},{7,6},{8,9},{9,8},{10,11... | collective-permute-start | bytes 2359304 | tf_op jit(solution)/shard_map/ppermute | solution.py:341
  78.0 17.0 %all-to-all-start.1 = ((f32[128,1,128]{2,1,0:T(1,128)}), f32[128,1,128]{2,1,0:T(1,128)S(1)}, u32[]{:S(2)}, u32[]{:S(2)}) async-start(f32[128,1,128]{2,1,0:T(1,128)} %bitcast.3), calls=%async_computation.1 | async-start | bytes 131072 | tf_op jit(solution)/shard_map/all_to_all | solution.py:324

commit v5 on v4

--- a/solution.py
+++ b/solution.py
@@ -18,6 +18,7 @@
 ABSENT = 64.0
 NEG = -1e30
 HUGE = 1e37
+TINY = 1e-25
 LN2 = math.log(2.0)
 TO_LOG2 = 0.0625 / LN2
 
@@ -136,117 +137,92 @@
 CHUNK = 256
 
 
-def fill_bias(c_ref, bias_ref):
-    count = jnp.zeros((1, 1), F32)
+def eights(x, op):
+    return op(x.reshape(x.shape[0] // 8, 8, x.shape[1]), axis=0)
+
+
+def zeroed(c_ref, lo_ref):
+    gone = jnp.zeros((8, HALF), F32)
     for k in range(SLOTS // CHUNK):
         at = slice(k * CHUNK, (k + 1) * CHUNK)
-        absent = c_ref[at, 0:1].astype(F32) == ABSENT
-        bias_ref[at, :] = jnp.broadcast_to(jnp.where(absent, NEG, 0.0), (CHUNK, HALF))
-        count = count + jnp.sum(jnp.where(absent, 0.0, 1.0), axis=0, keepdims=True)
-    return count
-
-
-def log2_scores(q, c_ref, bias_ref, at):
-    bias = bias_ref[at, :]
-    return dot_nt(c_ref[at, :], q) * TO_LOG2 + jnp.concatenate([bias, bias], axis=1)
-
-
-def eights(x, op):
-    return op(x.reshape(x.shape[0] // 8, 8, x.shape[1]), axis=0)
-
-
-def sums(q, c_ref, bias_ref, top, first):
+        x = c_ref[at, :HALF].astype(F32)
+        absent = x == ABSENT
+        lo_ref[at, :] = jnp.where(absent, 0.0, x).astype(BF16)
+        gone = gone + eights(jnp.where(absent, 1.0, 0.0), jnp.sum)
+    return jnp.sum(jnp.sum(gone, axis=0, keepdims=True), axis=1, keepdims=True)
+
+
+def sums(q, c_ref, lo_ref):
     total = jnp.zeros((8, COLS), F32)
-    for at in range(first, SLOTS, CHUNK):
-        t = log2_scores(q, c_ref, bias_ref, slice(at, at + CHUNK))
-        total = total + eights(jnp.exp2(t - top), jnp.sum)
+    for k in range(SLOTS // CHUNK):
+        at = slice(k * CHUNK, (k + 1) * CHUNK)
+        rows = jnp.concatenate([lo_ref[at, :], c_ref[at, HALF:]], axis=1)
+        total = total + eights(jnp.exp2(dot_nt(rows, q) * TO_LOG2), jnp.sum)
     return jnp.sum(total, axis=0, keepdims=True)
 
 
-def exact(q_ref, c_ref, bias_ref, t_ref, done):
+def exact(q_ref, c_refs, t_ref, lse_ref):
+    steps = SLOTS // CHUNK
+
     def block(j, _):
         cols = pl.ds(pl.multiple_of(j * COLS, COLS), COLS)
         q = q_ref[cols, :]
-
-        def scores(k, top):
-            at = pl.ds(pl.multiple_of(k * CHUNK, CHUNK), CHUNK)
-            t = log2_scores(q, c_ref, bias_ref, at)
-            t_ref[at, :] = t
-            return jnp.maximum(top, eights(t, jnp.max))
-
-        top = lax.fori_loop(0, SLOTS // CHUNK, scores, jnp.full((8, COLS), 2 * NEG, F32))
+        top = jnp.full((8, COLS), 2 * NEG, F32)
+        for i, c_ref in enumerate(c_refs):
+
+            def scores(k, top):
+                at = pl.ds(pl.multiple_of(k * CHUNK, CHUNK), CHUNK)
+                rows = c_ref[at, :]
+                absent = rows[:, 0:1].astype(F32) == ABSENT
+                t = dot_nt(rows, q) * TO_LOG2 + jnp.where(absent, NEG, 0.0)
+                t_ref[i, at, :] = t
+                return jnp.maximum(top, eights(t, jnp.max))
+
+            top = lax.fori_loop(0, steps, scores, top)
         top = jnp.max(top, axis=0, keepdims=True)
-
-        def add(k, total):
-            at = pl.ds(pl.multiple_of(k * CHUNK, CHUNK), CHUNK)
-            return total + eights(jnp.exp2(t_ref[at, :] - top), jnp.sum)
-
-        total = lax.fori_loop(0, SLOTS // CHUNK, add, jnp.zeros((8, COLS), F32))
-        done(cols, top, jnp.sum(total, axis=0, keepdims=True))
+        total = jnp.zeros((8, COLS), F32)
+        for i in range(len(c_refs)):
+
+            def add(k, total):
+                at = pl.ds(pl.multiple_of(k * CHUNK, CHUNK), CHUNK)
+                return total + eights(jnp.exp2(t_ref[i, at, :] - top), jnp.sum)
+
+            total = lax.fori_loop(0, steps, add, total)
+        lse_ref[:, cols] = top * LN2 + jnp.log(jnp.sum(total, axis=0, keepdims=True))
         return 0
 
     lax.fori_loop(0, SLOTS // COLS, block, 0)
 
 
-def too_large(totals):
-    worst = totals[0]
-    for total in totals[1:]:
-        worst = jnp.maximum(worst, total)
-    return jnp.max(worst) > HUGE
-
-
-def own_kernel(in_ref, c_ref, q_ref, top_ref, total_ref, count_ref, bias_ref, t_ref):
+def own_kernel(in_ref, c_ref, q_ref, total_ref, gone_ref, lo_ref):
     main_rows(in_ref, 32, q_ref)
     rest_rows(in_ref, True, q_ref)
-    count_ref[...] = jnp.broadcast_to(fill_bias(c_ref, bias_ref), (1, 128))
-    totals = []
-    top = None
-    for j in range(SLOTS // COLS + 1):
-        if j < SLOTS // COLS:
-            kept = slice((j % 2) * CHUNK, (j % 2 + 1) * CHUNK)
-            t = log2_scores(q_ref[j * COLS : (j + 1) * COLS, :], c_ref, bias_ref, slice(0, CHUNK))
-            t_ref[kept, :] = t
-            next_top = jnp.max(eights(t, jnp.max), axis=0, keepdims=True)
-        if j > 0:
-            cols = slice((j - 1) * COLS, j * COLS)
-            kept = slice(((j - 1) % 2) * CHUNK, ((j - 1) % 2 + 1) * CHUNK)
-            total = jnp.sum(eights(jnp.exp2(t_ref[kept, :] - top), jnp.sum), axis=0, keepdims=True)
-            total = total + sums(q_ref[cols, :], c_ref, bias_ref, top, CHUNK)
-            top_ref[:, cols] = top
-            total_ref[:, cols] = total
-            totals.append(total)
-        top = next_top
-
-    @pl.when(too_large(totals))
-    def _():
-        def done(cols, top, total):
-            top_ref[:, cols] = top
-            total_ref[:, cols] = total
-
-        exact(q_ref, c_ref, bias_ref, t_ref, done)
-
-
-def other_kernel(
-    q_ref, c_ref, top_ref, total_ref, count_ref, out_ref, lse_ref, n_ref, bias_ref, t_ref
-):
-    count = fill_bias(c_ref, bias_ref) + count_ref[:, 0:1]
-    totals = []
+    gone_ref[...] = jnp.broadcast_to(zeroed(c_ref, lo_ref), (1, 128))
     for j in range(SLOTS // COLS):
         cols = slice(j * COLS, (j + 1) * COLS)
-        top = top_ref[:, cols]
-        total = sums(q_ref[cols, :], c_ref, bias_ref, top, 0)
-        lse_ref[:, cols] = top * LN2 + jnp.log(total_ref[:, cols] + total)
-        totals.append(total)
-
-    @pl.when(too_large(totals))
+        total_ref[:, cols] = sums(q_ref[cols, :], c_ref, lo_ref)
+
+
+def other_kernel(
+    q_ref, own_ref, c_ref, total_ref, gone_ref, out_ref, lse_ref, n_ref, lo_ref, t_ref
+):
+    gone = zeroed(c_ref, lo_ref) + gone_ref[:, 0:1]
+    count = 2 * SLOTS - gone
+    most = least = None
+    for j in range(SLOTS // COLS):
+        cols = slice(j * COLS, (j + 1) * COLS)
+        total = total_ref[:, cols] + sums(q_ref[cols, :], c_ref, lo_ref)
+        present = total - gone
+        lse_ref[:, cols] = jnp.log(jnp.maximum(present, TINY))
+        most = total if j == 0 else jnp.maximum(most, total)
+        least = present if j == 0 else jnp.minimum(least, present)
+    most = jnp.max(most, axis=1, keepdims=True)
+    least = jnp.min(least, axis=1, keepdims=True)
+    redo = (count > 0) & ((most > HUGE) | (least < 0.25 * gone + TINY))
+
+    @pl.when(jnp.max(jnp.where(redo, 1.0, 0.0)) > 0)
     def _():
-        def done(cols, top, total):
-            top0 = top_ref[:, cols]
-            new = jnp.maximum(top0, top)
-            both = total_ref[:, cols] * jnp.exp2(top0 - new) + total * jnp.exp2(top - new)
-            lse_ref[:, cols] = new * LN2 + jnp.log(both)
-
-        exact(q_ref, c_ref, bias_ref, t_ref, done)
+        exact(q_ref, (own_ref, c_ref), t_ref, lse_ref)
 
     n = jnp.broadcast_to(count, (1, 128))
     n_ref[...] = n
@@ -341,14 +317,15 @@
     other_c = lax.ppermute(own_c, "rep", [(0, 1), (1, 0)])
     line = shape((1, SLOTS), F32)
     short = shape((1, 128), F32)
-    scratch = [pltpu.VMEM((SLOTS, HALF), F32), pltpu.VMEM((SLOTS, COLS), F32)]
-    own_q, top, total, count = call(
-        own_kernel, "own", (shape((SLOTS, WIDTH), BF16), line, line, short),
-        received, own_c, scratch=scratch,
+    low = pltpu.VMEM((SLOTS, HALF), BF16)
+    own_q, total, gone = call(
+        own_kernel, "own", (shape((SLOTS, WIDTH), BF16), line, short),
+        received, own_c, scratch=[low],
     )
     back, lse, n = call(
         other_kernel, "other", (shape((PEERS, 128), F32), line, short),
-        own_q, other_c, top, total, count, scratch=scratch,
+        own_q, own_c, other_c, total, gone,
+        scratch=[low, pltpu.VMEM((2, SLOTS, COLS), F32)],
     )
     returned = exchange(back)
     pos, hot, lane = call(

time: 97.3 us -> 107 us (1.100)
  Pallas kernels: 19.9 us -> 29.1 us
    pallas_call x7, Pallas kernels: 19.9 us -> 29.1 us  [call(): pl.pallas_call(kernel, out_shape=out_shape, in_specs=specs or [VMEM] * le...]
  transfers between devices with their start and end apart: 2 -> 2, of which waited for: 1 -> 2; matrix products, arithmetic and copies ran while one was open for 0% -> 0% of each run, Pallas kernels for 14% -> 3%
where the time goes in v5:
time: 107 us; the launch traced here: 106 us
  blocking collectives  58.6 us (55%)
  Pallas kernels  29.1 us (27%)
  starting transfers between devices  10.2 us (10%)
  waiting for transfers between devices  5.93 us (6%)
  between operations  2.52 us (2%)
    all_to_all x1, blocking collectives, exchange(): return lax.all_to_all(x, 'dp', split_axis=0, concat_axis=0, tiled=True)  55.3 us
    pallas_call x7, Pallas kernels, call(): pl.pallas_call(kernel, out_shape=out_shape, in_specs=specs or [VMEM] * le...  29.1 us
    all_to_all x1, starting transfers between devices, exchange(): return lax.all_to_all(x, 'dp', split_axis=0, concat_axis=0, tiled=True)  6.17 us
    all_to_all x1, waiting for transfers between devices, exchange(): return lax.all_to_all(x, 'dp', split_axis=0, concat_axis=0, tiled=True)  5.79 us
    ppermute x1, starting transfers between devices, shards(): other_c = lax.ppermute(own_c, 'rep', [(0, 1), (1, 0)])  4.03 us
    psum x1, blocking collectives, shards(): loss_total = lax.psum(loss_sum[0, 0], 'rep')  3.26 us
  transfers between devices with their start and end apart: 2, of which 2 were waited for; matrix products, arithmetic and copies ran while one was open for 0% of the time, Pallas kernels for 3%

profile of v5, /device:TPU:1, one launch (start us, length us, event | category | flops | bytes accessed | tf_op | source)
XLA Modules:
  0.0 106.3 jit_solution(10779152111254138940)
XLA Ops:
  0.6 2.6 %pack.1 = bf16[128,48,128]{2,1,0:T(8,128)(2,1)S(1)} custom-call(s32[1,768]{1,0:T(1,128)} %bitcast.13, bf16[768,256]{1,0:T(8,128)(2,1)} %q_hbm.1, bf16[768,256]{1,0:T(8,128)(2,1)} %c_hbm.1), custom_call_target="tpu_custom_call" | custom-call | tf_op jit(solution)/shard_map/pack/pallas_call | solution.py:288
  3.2 55.3 %all_to_all.16.in_ref = bf16[128,48,128]{2,1,0:T(8,128)(2,1)S(1)} all-to-all(bf16[128,48,128]{2,1,0:T(8,128)(2,1)S(1)} %pack.1), channel_id=1, replica_groups=mesh['dp'=128,'rep'=2] {'dp'}, dimensions={0} | all-to-all | bytes 3145728 | tf_op jit(solution)/shard_map/all_to_all | solution.py:300
  58.5 0.2 candidates.1.c_ref.own_ref
  58.7 4.0 %collective-permute-start = (bf16[1536,256]{1,0:T(8,128)(2,1)S(1)}, bf16[1536,256]{1,0:T(8,128)(2,1)S(1)}, u32[]{:S(2)}, u32[]{:S(2)}) collective-permute-start(bf16[1536,256]{1,0:T(8,128)(2,1)S(1)} %candidates.1.c_ref.own_ref), channel_id=1, source_target_pairs={{0,1},{1,0},{2,3},{3,2},{4,5},{5,4},{6,7},{7,6},{8,9},{9,8},{10,11... | collective-permute-start | bytes 2359304 | tf_op jit(solution)/shard_map/ppermute | solution.py:317
  62.8 1.8 %own.1 = (bf16[1536,256]{1,0:T(8,128)(2,1)S(1)}, f32[1,1536]{1,0:T(1,128)S(1)}, f32[1,128]{1,0:T(1,128)S(1)}) custom-call(bf16[128,48,128]{2,1,0:T(8,128)(2,1)S(1)} %all_to_all.16.in_ref, bf16[1536,256]{1,0:T(8,128)(2,1)S(1)} %candidates.1.c_ref.own_ref), custom_call_target="tpu_custom_call" | custom-call | tf_op jit(solution)/shard_map/own/pallas_call | solution.py:288
  64.5 0.0 copy-start
  64.5 0.0 copy-start.1
  64.5 0.0 copy-start.2
  64.5 0.1 collective-permute-done.c_ref
  64.7 22.6 %other.1 = (f32[128,128]{1,0:T(8,128)}, f32[1,1536]{1,0:T(1,128)S(1)}, f32[1,128]{1,0:T(1,128)S(1)}) custom-call(bf16[1536,256]{1,0:T(8,128)(2,1)S(1)} %get-tuple-element.14.q_ref, bf16[1536,256]{1,0:T(8,128)(2,1)S(1)} %candidates.1.c_ref.own_ref, bf16[1536,256]{1,0:T(8,128)(2,1)S(1)} %collective-permute-done.c_ref, ...), custom_call_target="tpu_custom_call" | custom-call | tf_op jit(solution)/shard_map/other/pallas_call | solution.py:288
  87.3 6.2 %all-to-all-start.1 = ((f32[128,1,128]{2,1,0:T(1,128)}), f32[128,1,128]{2,1,0:T(1,128)S(1)}, u32[]{:S(2)}, u32[]{:S(2)}) async-start(f32[128,1,128]{2,1,0:T(1,128)} %bitcast.3), calls=%async_computation.1 | async-start | bytes 131072 | tf_op jit(solution)/shard_map/all_to_all | solution.py:300
  93.5 0.0 copy-done
  93.5 0.0 copy-done.1
  93.5 0.0 copy-done.2
  93.5 0.5 positive.1
  94.0 0.5 sum.1
  94.5 3.3 %psum.7 = f32[]{:T(128)} all-reduce(f32[]{:T(128)S(1)} %bitcast.16), channel_id=1, replica_groups=mesh['dp'=128,'rep'=2] {'rep'}, use_global_device_ids=true, to_apply=%region_0.0 | all-reduce | flops 1 | bytes 8 | tf_op jit(solution)/shard_map/psum | solution.py:337
  98.5 5.8 %all-to-all-done.1 = f32[128,1,128]{2,1,0:T(1,128)S(1)} async-done(((f32[128,1,128]{2,1,0:T(1,128)}), f32[128,1,128]{2,1,0:T(1,128)S(1)}, u32[]{:S(2)}, u32[]{:S(2)}) %all-to-all-start.1) | async-done | bytes 65568 | tf_op jit(solution)/shard_map/all_to_all | solution.py:300
  104.2 1.0 finish.1
Async XLA Ops:
  58.7 5.9 %collective-permute-start = (bf16[1536,256]{1,0:T(8,128)(2,1)S(1)}, bf16[1536,256]{1,0:T(8,128)(2,1)S(1)}, u32[]{:S(2)}, u32[]{:S(2)}) collective-permute-start(bf16[1536,256]{1,0:T(8,128)(2,1)S(1)} %candidates.1.c_ref.own_ref), channel_id=1, source_target_pairs={{0,1},{1,0},{2,3},{3,2},{4,5},{5,4},{6,7},{7,6},{8,9},{9,8},{10,11... | collective-permute-start | bytes 2359304 | tf_op jit(solution)/shard_map/ppermute | solution.py:317
  64.5 29.0 %copy-start = (bf16[768,256]{1,0:T(8,128)(2,1)S(1)}, bf16[768,256]{1,0:T(8,128)(2,1)}, u32[]{:S(2)}) copy-start(bf16[768,256]{1,0:T(8,128)(2,1)} %q_hbm.1) | copy-start | bytes 1179652
  64.5 29.0 %copy-start.1 = (bf16[768,256]{1,0:T(8,128)(2,1)S(1)}, bf16[768,256]{1,0:T(8,128)(2,1)}, u32[]{:S(2)}) copy-start(bf16[768,256]{1,0:T(8,128)(2,1)} %c_hbm.1) | copy-start | bytes 1179652
  64.5 29.0 %copy-start.2 = (s32[768,1]{0,1:T(1,128)S(1)}, s32[768,1]{0,1:T(1,128)}, u32[]{:S(2)}) copy-start(s32[768,1]{0,1:T(1,128)} %param.5) | copy-start | bytes 9220
  87.3 16.9 %all-to-all-start.1 = ((f32[128,1,128]{2,1,0:T(1,128)}), f32[128,1,128]{2,1,0:T(1,128)S(1)}, u32[]{:S(2)}, u32[]{:S(2)}) async-start(f32[128,1,128]{2,1,0:T(1,128)} %bitcast.3), calls=%async_computation.1 | async-start | bytes 131072 | tf_op jit(solution)/shard_map/all_to_all | solution.py:300

commit v6 on v5

--- a/solution.py
+++ b/solution.py
@@ -6,6 +6,7 @@
 from jax.experimental import pallas as pl
 from jax.experimental.pallas import tpu as pltpu
 from jax.sharding import PartitionSpec as P
+
 
 ROWS = 768
 WIDTH = 256
@@ -59,7 +60,9 @@
     return jnp.concatenate(rank, axis=1).astype(jnp.int32), before
 
 
-def pack_kernel(b_hbm, q_hbm, c_hbm, out_ref, b_ref, q_ref, c_ref, b_sem, q_sem, c_sem):
+def pack_kernel(
+    b_hbm, q_hbm, c_hbm, out_ref, rank_ref, pos_ref, b_ref, q_ref, c_ref, b_sem, q_sem, c_sem
+):
     load_b = pltpu.make_async_copy(b_hbm, b_ref, b_sem)
     load_c = pltpu.make_async_copy(c_hbm, c_ref, c_sem)
     load_q = pltpu.make_async_copy(q_hbm, q_ref, q_sem)
@@ -69,6 +72,7 @@
     load_b.wait()
     b = b_ref[...]
     rank, count = ranks(b)
+    rank_ref[...] = rank
     count = count.astype(jnp.int32)
     main_key = jnp.where(rank < 8, b * 8 + rank, -1)
     rest_key = jnp.where(rank >= 8, b * 4 + rank - 8, -1)
@@ -106,6 +110,11 @@
         out_ref[p0 : p0 + step, 32:48, :] = jnp.concatenate(
             [q_main[:, :, :HALF], q_main[:, :, HALF:]], axis=1
         ).astype(BF16)
+    both = q.astype(F32) * c.astype(F32)
+    hi = both.astype(BF16)
+    lo = (both - hi.astype(F32)).astype(BF16)
+    ones = jnp.ones((8, WIDTH), BF16)
+    pos_ref[...] = ((dot_nt(ones, hi) + dot_nt(ones, lo)) * 0.0625)[0:1]
 
 
 def main_rows(in_ref, at, ref):
@@ -194,17 +203,22 @@
     lax.fori_loop(0, SLOTS // COLS, block, 0)
 
 
-def own_kernel(in_ref, c_ref, q_ref, total_ref, gone_ref, lo_ref):
+def own_kernel(in_ref, c_ref, q_ref, total_ref, gone_ref, pos_ref, lo_ref):
     main_rows(in_ref, 32, q_ref)
     rest_rows(in_ref, True, q_ref)
     gone_ref[...] = jnp.broadcast_to(zeroed(c_ref, lo_ref), (1, 128))
     for j in range(SLOTS // COLS):
         cols = slice(j * COLS, (j + 1) * COLS)
         total_ref[:, cols] = sums(q_ref[cols, :], c_ref, lo_ref)
+    pos = jnp.zeros((8, WIDTH), F32)
+    for k in range(SLOTS // CHUNK):
+        at = slice(k * CHUNK, (k + 1) * CHUNK)
+        pos = pos + eights(q_ref[at, :].astype(F32) * c_ref[at, :].astype(F32), jnp.sum)
+    pos_ref[...] = jnp.sum(pos, axis=0, keepdims=True)[:, :HALF] + jnp.sum(pos, axis=0, keepdims=True)[:, HALF:]
 
 
 def other_kernel(
-    q_ref, own_ref, c_ref, total_ref, gone_ref, out_ref, lse_ref, n_ref, lo_ref, t_ref
+    q_ref, own_ref, c_ref, total_ref, gone_ref, pos_ref, out_ref, sum_ref, n_ref, lo_ref, t_ref, lse_ref
 ):
     gone = zeroed(c_ref, lo_ref) + gone_ref[:, 0:1]
     count = 2 * SLOTS - gone
@@ -228,8 +242,11 @@
     n_ref[...] = n
     log_n = jnp.log(jnp.maximum(n, 1.0))
     lines = [lse_ref[:, t * 128 : (t + 1) * 128] - log_n for t in range(CAP)]
-    for t in range(CAP):
-        lse_ref[:, t * 128 : (t + 1) * 128] = lines[t]
+    loss = lines[0]
+    for line in lines[1:]:
+        loss = loss + line
+    loss = jnp.sum(loss - pos_ref[...] * 0.0625, axis=1, keepdims=True)
+    sum_ref[...] = jnp.broadcast_to(jnp.where(count > 0, loss, 0.0), (1, 128))
     lane = iota((1, 128), 1)
     for u in range(PEERS // 8):
         a = lines[u // 2]
@@ -243,47 +260,24 @@
         out_ref[u * 8 : (u + 1) * 8, :] = jnp.broadcast_to(line, (8, 128))
 
 
-def sum_kernel(in_ref, lse_ref, n_ref, sum_ref):
-    total = jnp.sum(lse_ref[...], axis=1, keepdims=True)
-    total = jnp.where(n_ref[:, 0:1] > 0, total, 0.0)
-    c = in_ref[:, 0:16, :].astype(F32)
-    q = in_ref[:, 32:48, :].astype(F32)
-    pos = jnp.sum(c * q, axis=0)
-    z = in_ref[:, 16:32, :].astype(F32).reshape(PEERS * 2, 8, HALF)
-    low = iota((PEERS * 2, 8, HALF), 1) < 4
-    rest = jnp.sum(jnp.where(low, z * pltpu.roll(z, 4, 1), 0.0), axis=0)
-    pos = jnp.sum(jnp.sum(pos, axis=0, keepdims=True), axis=1, keepdims=True)
-    rest = jnp.sum(jnp.sum(rest, axis=0, keepdims=True), axis=1, keepdims=True)
-    sum_ref[...] = jnp.broadcast_to(total - (pos + rest) * 0.0625, (1, 128))
-
-
-def positive_kernel(at_ref, b_ref, q_ref, c_ref, pos_ref, hot_ref, lane_ref):
-    rank, _ = ranks(b_ref[...])
-    eighth = at_ref[0] & 7
-    lane_ref[...] = jnp.where(rank < 8, eighth * 8 + rank, 64 + eighth * 4 + rank - 8)
-    hot_ref[...] = (iota((PEERS, ROWS), 0) == b_ref[...]).astype(F32).astype(BF16)
-    both = q_ref[...].astype(F32) * c_ref[...].astype(F32)
-    hi = both.astype(BF16)
-    lo = (both - hi.astype(F32)).astype(BF16)
-    ones = jnp.ones((8, WIDTH), BF16)
-    pos_ref[...] = ((dot_nt(ones, hi) + dot_nt(ones, lo)) * 0.0625)[0:1]
-
-
-def finish_kernel(hot_ref, lane_ref, pos_ref, back_ref, out_ref):
-    hot = hot_ref[...]
+def finish_kernel(b_ref, rank_ref, pos_ref, back_ref, out_ref):
+    eighth = lax.axis_index("dp") & 7
+    rank = rank_ref[...]
+    lane = jnp.where(rank < 8, eighth * 8 + rank, 64 + eighth * 4 + rank - 8)
+    hot = (iota((PEERS, ROWS), 0) == b_ref[...]).astype(F32).astype(BF16)
     x = back_ref[...]
     hi = x.astype(BF16)
     left = x - hi.astype(F32)
     mid = left.astype(BF16)
     lo = (left - mid.astype(F32)).astype(BF16)
     picked = (dot_tn(hi, hot) + dot_tn(mid, hot)) + dot_tn(lo, hot)
-    mine = jnp.where(iota((128, ROWS), 0) == lane_ref[...], picked, 0.0)
+    mine = jnp.where(iota((128, ROWS), 0) == lane, picked, 0.0)
     mine = jnp.sum(mine, axis=0, keepdims=True) - pos_ref[...]
     for j in range(ROWS // 128):
         out_ref[j : j + 1, :] = mine[:, j * 128 : (j + 1) * 128]
 
 
-def call(kernel, name, out_shape, *args, specs=None, scratch=()):
+def call(kernel, out_shape, *args, specs=None, scratch=()):
     single = not isinstance(out_shape, tuple)
     return pl.pallas_call(
         kernel,
@@ -292,7 +286,6 @@
         out_specs=VMEM if single else (VMEM,) * len(out_shape),
         scratch_shapes=scratch,
         compiler_params=pltpu.CompilerParams(vmem_limit_bytes=24 * 1024 * 1024),
-        name=name,
     )(*args)
 
 
@@ -300,49 +293,41 @@
     return lax.all_to_all(x, "dp", split_axis=0, concat_axis=0, tiled=True)
 
 
-def shards(queries, candidates, bucket):
+def steps(queries, candidates, bucket):
     b = bucket.reshape(1, ROWS)
-    me = lax.axis_index("dp").astype(jnp.int32).reshape(1)
     shape = jax.ShapeDtypeStruct
     hbm = pl.BlockSpec(memory_space=pltpu.HBM)
     rows = pltpu.VMEM((ROWS, WIDTH), BF16)
-    packed = call(
-        pack_kernel, "pack", shape((PEERS, 48, HALF), BF16),
+    packed, rank, pos = call(
+        pack_kernel,
+        (shape((PEERS, 48, HALF), BF16), shape((1, ROWS), jnp.int32), shape((1, ROWS), F32)),
         *[pltpu.with_memory_space_constraint(x, pltpu.HBM) for x in (b, queries, candidates)],
         specs=[hbm] * 3,
         scratch=[pltpu.VMEM((1, ROWS), jnp.int32), rows, rows] + [pltpu.SemaphoreType.DMA] * 3,
     )
     received = exchange(packed)
-    own_c = call(candidates_kernel, "candidates", shape((SLOTS, WIDTH), BF16), received)
+    own_c = call(candidates_kernel, shape((SLOTS, WIDTH), BF16), received)
     other_c = lax.ppermute(own_c, "rep", [(0, 1), (1, 0)])
     line = shape((1, SLOTS), F32)
     short = shape((1, 128), F32)
     low = pltpu.VMEM((SLOTS, HALF), BF16)
-    own_q, total, gone = call(
-        own_kernel, "own", (shape((SLOTS, WIDTH), BF16), line, short),
+    own_q, total, gone, pos_sum = call(
+        own_kernel, (shape((SLOTS, WIDTH), BF16), line, short, short),
         received, own_c, scratch=[low],
     )
-    back, lse, n = call(
-        other_kernel, "other", (shape((PEERS, 128), F32), line, short),
-        own_q, own_c, other_c, total, gone,
-        scratch=[low, pltpu.VMEM((2, SLOTS, COLS), F32)],
+    back, loss_sum, n = call(
+        other_kernel, (shape((PEERS, 128), F32), short, short),
+        own_q, own_c, other_c, total, gone, pos_sum,
+        scratch=[low, pltpu.VMEM((2, SLOTS, COLS), F32), pltpu.VMEM((1, SLOTS), F32)],
     )
+    other_sum = lax.ppermute(loss_sum, "rep", [(0, 1), (1, 0)])
     returned = exchange(back)
-    pos, hot, lane = call(
-        positive_kernel, "positive",
-        (shape((1, ROWS), F32), shape((PEERS, ROWS), BF16), shape((1, ROWS), jnp.int32)),
-        me, b, queries, candidates, specs=[pl.BlockSpec(memory_space=pltpu.SMEM)] + [VMEM] * 3,
-    )
-    loss_sum = call(sum_kernel, "sum", short, received, lse, n)
-    loss_total = lax.psum(loss_sum[0, 0], "rep")
-    bucket_loss = (loss_total / jnp.maximum(n[0, 0], 1.0)).reshape(1)
-    query_loss = call(
-        finish_kernel, "finish", shape((ROWS // 128, 128), F32), hot, lane, pos, returned
-    )
-    return (query_loss.reshape(ROWS), bucket_loss)
+    query_loss = call(finish_kernel, shape((ROWS // 128, 128), F32), b, rank, pos, returned)
+    mean = (loss_sum + other_sum) / jnp.maximum(n, 1.0)
+    return (query_loss.reshape(ROWS), mean[0, 0:1])
 
 
 def solution(mesh):
     in_specs = (P(("dp", "rep"), None), P(("dp", "rep"), None), P(("dp", "rep"), None))
     out_specs = (P(("dp", "rep")), P("dp"))
-    return jax.shard_map(shards, mesh=mesh, in_specs=in_specs, out_specs=out_specs, check_vma=False)
+    return jax.shard_map(steps, mesh=mesh, in_specs=in_specs, out_specs=out_specs, check_vma=False)

time: 107 us -> 106 us (level)
  waiting for transfers between devices: 5.93 us -> 10.4 us
  blocking collectives: 58.6 us -> 55.3 us
  between operations: 2.52 us -> 0.67 us
    all_to_all x1, waiting for transfers between devices: 5.79 us -> 10.3 us  [exchange(): return lax.all_to_all(x, 'dp', split_axis=0, concat_axis=0, tiled=True)]
    psum x1 -> x0, blocking collectives: 3.26 us -> none  [shards(): loss_total = lax.psum(loss_sum[0, 0], 'rep')]
    pallas_call x7 -> x5, Pallas kernels: 29.1 us -> 28.5 us  [call(): pl.pallas_call(kernel, out_shape=out_shape, in_specs=specs or [VMEM] * le...]
    ppermute x1 -> x2, starting transfers between devices: 4.03 us -> 4.44 us  [the longest x1 4.06 us: steps(): other_c = lax.ppermute(own_c, 'rep', [(0, 1), (1, 0)])]
  transfers between devices with their start and end apart: 2 -> 3, of which waited for: 2 -> 2; matrix products, arithmetic and copies ran while one was open for 0% -> 0% of each run, Pallas kernels for 3% -> 2%
where the time goes in v6:
time: 106 us
  blocking collectives  55.3 us (52%)
  Pallas kernels  28.5 us (27%)
  starting transfers between devices  10.6 us (10%)
  waiting for transfers between devices  10.4 us (10%)
    all_to_all x1, blocking collectives, exchange(): return lax.all_to_all(x, 'dp', split_axis=0, concat_axis=0, tiled=True)  55.3 us
    pallas_call x5, Pallas kernels, call(): pl.pallas_call(kernel, out_shape=out_shape, in_specs=specs or [VMEM] * le...  28.5 us
    all_to_all x1, waiting for transfers between devices, exchange(): return lax.all_to_all(x, 'dp', split_axis=0, concat_axis=0, tiled=True)  10.3 us
    all_to_all x1, starting transfers between devices, exchange(): return lax.all_to_all(x, 'dp', split_axis=0, concat_axis=0, tiled=True)  6.16 us
    ppermute x1, starting transfers between devices, steps(): other_c = lax.ppermute(own_c, 'rep', [(0, 1), (1, 0)])  4.06 us
  transfers between devices with their start and end apart: 3, of which 2 were waited for; matrix products, arithmetic and copies ran while one was open for 0% of the time, Pallas kernels for 2%

profile of v6, /device:TPU:1, one launch (start us, length us, event | category | flops | bytes accessed | tf_op | source)
XLA Modules:
  0.0 105.9 jit_solution(11837847986842171714)
XLA Ops:
  0.6 2.9 %shard_map.50 = (bf16[128,48,128]{2,1,0:T(8,128)(2,1)S(1)}, s32[1,768]{1,0:T(1,128)S(1)}, f32[1,768]{1,0:T(1,128)S(1)}) custom-call(s32[1,768]{1,0:T(1,128)} %bitcast.9, bf16[768,256]{1,0:T(8,128)(2,1)} %q_hbm.1, bf16[768,256]{1,0:T(8,128)(2,1)} %c_hbm.1), custom_call_target="tpu_custom_call" | custom-call | tf_op jit(solution)/shard_map/pallas_call | solution.py:282
  3.5 55.3 %all_to_all.16.in_ref = bf16[128,48,128]{2,1,0:T(8,128)(2,1)S(1)} all-to-all(bf16[128,48,128]{2,1,0:T(8,128)(2,1)S(1)} %get-tuple-element.14), channel_id=1, replica_groups=mesh['dp'=128,'rep'=2] {'dp'}, dimensions={0} | all-to-all | bytes 3145728 | tf_op jit(solution)/shard_map/all_to_all | solution.py:293
  58.8 0.2 shard_map.51.c_ref.own_ref
  59.0 4.1 %collective-permute-start = (bf16[1536,256]{1,0:T(8,128)(2,1)S(1)}, bf16[1536,256]{1,0:T(8,128)(2,1)S(1)}, u32[]{:S(2)}, u32[]{:S(2)}) collective-permute-start(bf16[1536,256]{1,0:T(8,128)(2,1)S(1)} %shard_map.51.c_ref.own_ref), channel_id=1, source_target_pairs={{0,1},{1,0},{2,3},{3,2},{4,5},{5,4},{6,7},{7,6},{8,9},{9,8},{10,11... | collective-permute-start | bytes 2359304 | tf_op jit(solution)/shard_map/ppermute | solution.py:310
  63.1 1.8 %shard_map.52 = (bf16[1536,256]{1,0:T(8,128)(2,1)S(1)}, f32[1,1536]{1,0:T(1,128)S(1)}, f32[1,128]{1,0:T(1,128)S(1)}, f32[1,128]{1,0:T(1,128)S(1)}) custom-call(bf16[128,48,128]{2,1,0:T(8,128)(2,1)S(1)} %all_to_all.16.in_ref, bf16[1536,256]{1,0:T(8,128)(2,1)S(1)} %shard_map.51.c_ref.own_ref), custom_call_target="tpu_custom_call" | custom-call | tf_op jit(solution)/shard_map/pallas_call | solution.py:282
  64.9 0.0 copy-start
  64.9 0.1 collective-permute-done.c_ref
  65.0 22.7 %shard_map.53 = (f32[128,128]{1,0:T(8,128)}, f32[1,128]{1,0:T(1,128)S(1)}, f32[1,128]{1,0:T(1,128)S(1)}) custom-call(bf16[1536,256]{1,0:T(8,128)(2,1)S(1)} %get-tuple-element.15.q_ref, bf16[1536,256]{1,0:T(8,128)(2,1)S(1)} %shard_map.51.c_ref.own_ref, bf16[1536,256]{1,0:T(8,128)(2,1)S(1)} %collective-permute-done.c_ref, ...), custom_call_target="tpu_custom_call" | custom-call | tf_op jit(solution)/shard_map/pallas_call | solution.py:282
  87.6 0.4 collective-permute-start.1
  88.0 6.2 %all-to-all-start.1 = ((f32[128,1,128]{2,1,0:T(1,128)}), f32[128,1,128]{2,1,0:T(1,128)S(1)}, u32[]{:S(2)}, u32[]{:S(2)}) async-start(f32[128,1,128]{2,1,0:T(1,128)} %bitcast.2), calls=%async_computation.1 | async-start | bytes 131072 | tf_op jit(solution)/shard_map/all_to_all | solution.py:293
  94.2 0.0 collective-permute-done.1
  94.2 0.5 maximum_divide_fusion
  94.7 10.3 %all-to-all-done.1 = f32[128,1,128]{2,1,0:T(1,128)S(1)} async-done(((f32[128,1,128]{2,1,0:T(1,128)}), f32[128,1,128]{2,1,0:T(1,128)S(1)}, u32[]{:S(2)}, u32[]{:S(2)}) %all-to-all-start.1) | async-done | bytes 65568 | tf_op jit(solution)/shard_map/all_to_all | solution.py:293
  105.0 0.0 copy-done
  105.0 1.0 shard_map.54
Async XLA Ops:
  59.0 6.0 %collective-permute-start = (bf16[1536,256]{1,0:T(8,128)(2,1)S(1)}, bf16[1536,256]{1,0:T(8,128)(2,1)S(1)}, u32[]{:S(2)}, u32[]{:S(2)}) collective-permute-start(bf16[1536,256]{1,0:T(8,128)(2,1)S(1)} %shard_map.51.c_ref.own_ref), channel_id=1, source_target_pairs={{0,1},{1,0},{2,3},{3,2},{4,5},{5,4},{6,7},{7,6},{8,9},{9,8},{10,11... | collective-permute-start | bytes 2359304 | tf_op jit(solution)/shard_map/ppermute | solution.py:310
  64.9 40.1 %copy-start = (s32[768,1]{0,1:T(1,128)S(1)}, s32[768,1]{0,1:T(1,128)}, u32[]{:S(2)}) copy-start(s32[768,1]{0,1:T(1,128)} %param.5) | copy-start | bytes 9220
  87.6 6.6 %collective-permute-start.1 = (f32[1,128]{1,0:T(1,128)S(1)}, f32[1,128]{1,0:T(1,128)S(1)}, u32[]{:S(2)}, u32[]{:S(2)}) collective-permute-start(f32[1,128]{1,0:T(1,128)S(1)} %get-tuple-element.20), channel_id=1, source_target_pairs={{0,1},{1,0},{2,3},{3,2},{4,5},{5,4},{6,7},{7,6},{8,9},{9,8},{10,11... | collective-permute-start | bytes 1544 | tf_op jit(solution)/shard_map/ppermute | solution.py:323
  88.0 17.0 %all-to-all-start.1 = ((f32[128,1,128]{2,1,0:T(1,128)}), f32[128,1,128]{2,1,0:T(1,128)S(1)}, u32[]{:S(2)}, u32[]{:S(2)}) async-start(f32[128,1,128]{2,1,0:T(1,128)} %bitcast.2), calls=%async_computation.1 | async-start | bytes 131072 | tf_op jit(solution)/shard_map/all_to_all | solution.py:293

commit v7 on v6

--- a/solution.py
+++ b/solution.py
@@ -61,7 +61,7 @@
 
 
 def pack_kernel(
-    b_hbm, q_hbm, c_hbm, out_ref, rank_ref, pos_ref, b_ref, q_ref, c_ref, b_sem, q_sem, c_sem
+    b_hbm, q_hbm, c_hbm, out_ref, rank_ref, b_ref, q_ref, c_ref, b_sem, q_sem, c_sem
 ):
     load_b = pltpu.make_async_copy(b_hbm, b_ref, b_sem)
     load_c = pltpu.make_async_copy(c_hbm, c_ref, c_sem)
@@ -110,11 +110,6 @@
         out_ref[p0 : p0 + step, 32:48, :] = jnp.concatenate(
             [q_main[:, :, :HALF], q_main[:, :, HALF:]], axis=1
         ).astype(BF16)
-    both = q.astype(F32) * c.astype(F32)
-    hi = both.astype(BF16)
-    lo = (both - hi.astype(F32)).astype(BF16)
-    ones = jnp.ones((8, WIDTH), BF16)
-    pos_ref[...] = ((dot_nt(ones, hi) + dot_nt(ones, lo)) * 0.0625)[0:1]
 
 
 def main_rows(in_ref, at, ref):
@@ -161,10 +156,10 @@
     return jnp.sum(jnp.sum(gone, axis=0, keepdims=True), axis=1, keepdims=True)
 
 
-def sums(q, c_ref, lo_ref):
+def sums(q, c_ref, lo_ref, chunk):
     total = jnp.zeros((8, COLS), F32)
-    for k in range(SLOTS // CHUNK):
-        at = slice(k * CHUNK, (k + 1) * CHUNK)
+    for k in range(SLOTS // chunk):
+        at = slice(k * chunk, (k + 1) * chunk)
         rows = jnp.concatenate([lo_ref[at, :], c_ref[at, HALF:]], axis=1)
         total = total + eights(jnp.exp2(dot_nt(rows, q) * TO_LOG2), jnp.sum)
     return jnp.sum(total, axis=0, keepdims=True)
@@ -203,18 +198,26 @@
     lax.fori_loop(0, SLOTS // COLS, block, 0)
 
 
-def own_kernel(in_ref, c_ref, q_ref, total_ref, gone_ref, pos_ref, lo_ref):
+def own_kernel(
+    in_ref, c_ref, home_q_ref, home_c_ref, q_ref, total_ref, gone_ref, pos_ref, home_ref, lo_ref
+):
     main_rows(in_ref, 32, q_ref)
     rest_rows(in_ref, True, q_ref)
     gone_ref[...] = jnp.broadcast_to(zeroed(c_ref, lo_ref), (1, 128))
     for j in range(SLOTS // COLS):
         cols = slice(j * COLS, (j + 1) * COLS)
-        total_ref[:, cols] = sums(q_ref[cols, :], c_ref, lo_ref)
+        total_ref[:, cols] = sums(q_ref[cols, :], c_ref, lo_ref, 2 * CHUNK)
     pos = jnp.zeros((8, WIDTH), F32)
     for k in range(SLOTS // CHUNK):
         at = slice(k * CHUNK, (k + 1) * CHUNK)
         pos = pos + eights(q_ref[at, :].astype(F32) * c_ref[at, :].astype(F32), jnp.sum)
-    pos_ref[...] = jnp.sum(pos, axis=0, keepdims=True)[:, :HALF] + jnp.sum(pos, axis=0, keepdims=True)[:, HALF:]
+    pos = jnp.sum(pos, axis=0, keepdims=True)
+    pos_ref[...] = pos[:, :HALF] + pos[:, HALF:]
+    both = home_q_ref[...].astype(F32) * home_c_ref[...].astype(F32)
+    hi = both.astype(BF16)
+    lo = (both - hi.astype(F32)).astype(BF16)
+    ones = jnp.ones((8, WIDTH), BF16)
+    home_ref[...] = ((dot_nt(ones, hi) + dot_nt(ones, lo)) * 0.0625)[0:1]
 
 
 def other_kernel(
@@ -225,7 +228,7 @@
     most = least = None
     for j in range(SLOTS // COLS):
         cols = slice(j * COLS, (j + 1) * COLS)
-        total = total_ref[:, cols] + sums(q_ref[cols, :], c_ref, lo_ref)
+        total = total_ref[:, cols] + sums(q_ref[cols, :], c_ref, lo_ref, CHUNK)
         present = total - gone
         lse_ref[:, cols] = jnp.log(jnp.maximum(present, TINY))
         most = total if j == 0 else jnp.maximum(most, total)
@@ -260,7 +263,7 @@
         out_ref[u * 8 : (u + 1) * 8, :] = jnp.broadcast_to(line, (8, 128))
 
 
-def finish_kernel(b_ref, rank_ref, pos_ref, back_ref, out_ref):
+def pick_kernel(b_ref, rank_ref, pos_ref, back_ref, out_ref):
     eighth = lax.axis_index("dp") & 7
     rank = rank_ref[...]
     lane = jnp.where(rank < 8, eighth * 8 + rank, 64 + eighth * 4 + rank - 8)
@@ -277,6 +280,11 @@
         out_ref[j : j + 1, :] = mine[:, j * 128 : (j + 1) * 128]
 
 
+def finish_kernel(mine_ref, sum_ref, other_ref, n_ref, out_ref, mean_ref):
+    out_ref[...] = mine_ref[...]
+    mean_ref[...] = (sum_ref[...] + other_ref[...]) / jnp.maximum(n_ref[...], 1.0)
+
+
 def call(kernel, out_shape, *args, specs=None, scratch=()):
     single = not isinstance(out_shape, tuple)
     return pl.pallas_call(
@@ -297,13 +305,13 @@
     b = bucket.reshape(1, ROWS)
     shape = jax.ShapeDtypeStruct
     hbm = pl.BlockSpec(memory_space=pltpu.HBM)
-    rows = pltpu.VMEM((ROWS, WIDTH), BF16)
-    packed, rank, pos = call(
-        pack_kernel,
-        (shape((PEERS, 48, HALF), BF16), shape((1, ROWS), jnp.int32), shape((1, ROWS), F32)),
+    rows = shape((ROWS, WIDTH), BF16)
+    ints = shape((1, ROWS), jnp.int32)
+    packed, rank, b_here, q_here, c_here = call(
+        pack_kernel, (shape((PEERS, 48, HALF), BF16), ints, ints, rows, rows),
         *[pltpu.with_memory_space_constraint(x, pltpu.HBM) for x in (b, queries, candidates)],
         specs=[hbm] * 3,
-        scratch=[pltpu.VMEM((1, ROWS), jnp.int32), rows, rows] + [pltpu.SemaphoreType.DMA] * 3,
+        scratch=[pltpu.SemaphoreType.DMA] * 3,
     )
     received = exchange(packed)
     own_c = call(candidates_kernel, shape((SLOTS, WIDTH), BF16), received)
@@ -311,9 +319,10 @@
     line = shape((1, SLOTS), F32)
     short = shape((1, 128), F32)
     low = pltpu.VMEM((SLOTS, HALF), BF16)
-    own_q, total, gone, pos_sum = call(
-        own_kernel, (shape((SLOTS, WIDTH), BF16), line, short, short),
-        received, own_c, scratch=[low],
+    own_q, total, gone, pos_sum, pos = call(
+        own_kernel,
+        (shape((SLOTS, WIDTH), BF16), line, short, short, shape((1, ROWS), F32)),
+        received, own_c, q_here, c_here, scratch=[low],
     )
     back, loss_sum, n = call(
         other_kernel, (shape((PEERS, 128), F32), short, short),
@@ -322,8 +331,11 @@
     )
     other_sum = lax.ppermute(loss_sum, "rep", [(0, 1), (1, 0)])
     returned = exchange(back)
-    query_loss = call(finish_kernel, shape((ROWS // 128, 128), F32), b, rank, pos, returned)
-    mean = (loss_sum + other_sum) / jnp.maximum(n, 1.0)
+    mine = call(pick_kernel, shape((ROWS // 128, 128), F32), b_here, rank, pos, returned)
+    query_loss, mean = call(
+        finish_kernel, (shape((ROWS // 128, 128), F32), short),
+        mine, loss_sum, other_sum, n,
+    )
     return (query_loss.reshape(ROWS), mean[0, 0:1])
 
 

time: 106 us -> 105 us (level)
    pallas_call x5 -> x6, Pallas kernels: 28.5 us -> 28.3 us  [call(): pl.pallas_call(kernel, out_shape=out_shape, in_specs=specs or [VMEM] * le...]
  transfers between devices with their start and end apart: 3 -> 3, of which waited for: 2 -> 1; matrix products, arithmetic and copies ran while one was open for 0% -> 0% of each run, Pallas kernels for 2% -> 2%
where the time goes in v7:
time: 105 us
  blocking collectives  55.3 us (53%)
  Pallas kernels  28.3 us (27%)
  starting transfers between devices  10.9 us (10%)
  waiting for transfers between devices  10.1 us (10%)
    all_to_all x1, blocking collectives, exchange(): return lax.all_to_all(x, 'dp', split_axis=0, concat_axis=0, tiled=True)  55.3 us
    pallas_call x6, Pallas kernels, call(): pl.pallas_call(kernel, out_shape=out_shape, in_specs=specs or [VMEM] * le...  28.3 us
    all_to_all x1, waiting for transfers between devices, exchange(): return lax.all_to_all(x, 'dp', split_axis=0, concat_axis=0, tiled=True)  10 us
    all_to_all x1, starting transfers between devices, exchange(): return lax.all_to_all(x, 'dp', split_axis=0, concat_axis=0, tiled=True)  6.16 us
    ppermute x1, starting transfers between devices, steps(): other_c = lax.ppermute(own_c, 'rep', [(0, 1), (1, 0)])  4.03 us
  transfers between devices with their start and end apart: 3, of which 1 were waited for; matrix products, arithmetic and copies ran while one was open for 0% of the time, Pallas kernels for 2%

profile of v7, /device:TPU:1, one launch (start us, length us, event | category | flops | bytes accessed | tf_op | source)
XLA Modules:
  0.0 105.3 jit_solution(2898858047025346862)
XLA Ops:
  0.6 2.6 %shard_map.50 = (bf16[128,48,128]{2,1,0:T(8,128)(2,1)S(1)}, s32[1,768]{1,0:T(1,128)S(1)}, s32[1,768]{1,0:T(1,128)S(1)}, bf16[768,256]{1,0:T(8,128)(2,1)S(1)}, bf16[768,256]{1,0:T(8,128)(2,1)S(1)}) custom-call(s32[1,768]{1,0:T(1,128)} %bitcast.9, bf16[768,256]{1,0:T(8,128)(2,1)} %q_hbm.1, bf16[768,256]{1,0:T(8,128)(2,1)} %c_hbm.1), custom_call_target="tpu_custom_call" | custom-call | tf_op jit(solution)/shard_map/pallas_call | solution.py:290
  3.2 55.3 %all_to_all.16.in_ref = bf16[128,48,128]{2,1,0:T(8,128)(2,1)S(1)} all-to-all(bf16[128,48,128]{2,1,0:T(8,128)(2,1)S(1)} %get-tuple-element.19), channel_id=1, replica_groups=mesh['dp'=128,'rep'=2] {'dp'}, dimensions={0} | all-to-all | bytes 3145728 | tf_op jit(solution)/shard_map/all_to_all | solution.py:301
  58.5 0.2 shard_map.51.c_ref.own_ref
  58.7 4.0 %collective-permute-start = (bf16[1536,256]{1,0:T(8,128)(2,1)S(1)}, bf16[1536,256]{1,0:T(8,128)(2,1)S(1)}, u32[]{:S(2)}, u32[]{:S(2)}) collective-permute-start(bf16[1536,256]{1,0:T(8,128)(2,1)S(1)} %shard_map.51.c_ref.own_ref), channel_id=1, source_target_pairs={{0,1},{1,0},{2,3},{3,2},{4,5},{5,4},{6,7},{7,6},{8,9},{9,8},{10,11... | collective-permute-start | bytes 2359304 | tf_op jit(solution)/shard_map/ppermute | solution.py:318
  62.8 1.9 %shard_map.52 = (bf16[1536,256]{1,0:T(8,128)(2,1)S(1)}, f32[1,1536]{1,0:T(1,128)S(1)}, f32[1,128]{1,0:T(1,128)S(1)}, f32[1,128]{1,0:T(1,128)S(1)}, f32[1,768]{1,0:T(1,128)S(1)}) custom-call(bf16[128,48,128]{2,1,0:T(8,128)(2,1)S(1)} %all_to_all.16.in_ref, bf16[1536,256]{1,0:T(8,128)(2,1)S(1)} %shard_map.51.c_ref.own_ref, ...), custom_call_target="tpu_custom_call" | custom-call | tf_op jit(solution)/shard_map/pallas_call | solution.py:290
  64.6 0.0 collective-permute-done.c_ref
  64.7 22.7 %shard_map.53 = (f32[128,128]{1,0:T(8,128)}, f32[1,128]{1,0:T(1,128)S(1)}, f32[1,128]{1,0:T(1,128)S(1)}) custom-call(bf16[1536,256]{1,0:T(8,128)(2,1)S(1)} %get-tuple-element.23.q_ref, bf16[1536,256]{1,0:T(8,128)(2,1)S(1)} %shard_map.51.c_ref.own_ref, bf16[1536,256]{1,0:T(8,128)(2,1)S(1)} %collective-permute-done.c_ref, ...), custom_call_target="tpu_custom_call" | custom-call | tf_op jit(solution)/shard_map/pallas_call | solution.py:290
  87.4 6.2 %all-to-all-start.1 = ((f32[128,1,128]{2,1,0:T(1,128)}), f32[128,1,128]{2,1,0:T(1,128)S(1)}, u32[]{:S(2)}, u32[]{:S(2)}) async-start(f32[128,1,128]{2,1,0:T(1,128)} %bitcast.2), calls=%async_computation.1 | async-start | bytes 131072 | tf_op jit(solution)/shard_map/all_to_all | solution.py:301
  93.5 0.7 collective-permute-start.1
  94.3 10.0 %all-to-all-done.1 = f32[128,1,128]{2,1,0:T(1,128)S(1)} async-done(((f32[128,1,128]{2,1,0:T(1,128)}), f32[128,1,128]{2,1,0:T(1,128)S(1)}, u32[]{:S(2)}, u32[]{:S(2)}) %all-to-all-start.1) | async-done | bytes 65568 | tf_op jit(solution)/shard_map/all_to_all | solution.py:301
  104.3 0.4 shard_map.54.mine_ref
  104.7 0.0 collective-permute-done.1.other_ref
  104.7 0.6 shard_map.55
Async XLA Ops:
  58.7 5.9 %collective-permute-start = (bf16[1536,256]{1,0:T(8,128)(2,1)S(1)}, bf16[1536,256]{1,0:T(8,128)(2,1)S(1)}, u32[]{:S(2)}, u32[]{:S(2)}) collective-permute-start(bf16[1536,256]{1,0:T(8,128)(2,1)S(1)} %shard_map.51.c_ref.own_ref), channel_id=1, source_target_pairs={{0,1},{1,0},{2,3},{3,2},{4,5},{5,4},{6,7},{7,6},{8,9},{9,8},{10,11... | collective-permute-start | bytes 2359304 | tf_op jit(solution)/shard_map/ppermute | solution.py:318
  87.4 16.9 %all-to-all-start.1 = ((f32[128,1,128]{2,1,0:T(1,128)}), f32[128,1,128]{2,1,0:T(1,128)S(1)}, u32[]{:S(2)}, u32[]{:S(2)}) async-start(f32[128,1,128]{2,1,0:T(1,128)} %bitcast.2), calls=%async_computation.1 | async-start | bytes 131072 | tf_op jit(solution)/shard_map/all_to_all | solution.py:301
  93.5 11.1 %collective-permute-start.1 = (f32[1,128]{1,0:T(1,128)S(1)}, f32[1,128]{1,0:T(1,128)S(1)}, u32[]{:S(2)}, u32[]{:S(2)}) collective-permute-start(f32[1,128]{1,0:T(1,128)S(1)} %get-tuple-element.28.sum_ref), channel_id=1, source_target_pairs={{0,1},{1,0},{2,3},{3,2},{4,5},{5,4},{6,7},{7,6},{8,9},{9,8},{10,11... | collective-permute-start | bytes 1544 | tf_op jit(solution)/shard_map/ppermute | solution.py:332
